TPU v7x, 512 devices: a whole 4x8x8 slice. The times are simulated.
512 devices in a mesh: tile: 64 (over y, z_hi, x), tm: 8 (over z_lo, core).
Axes of the slice: x: 4, y: 8, z: 8 (z_hi: 2, z_lo: 4; z = z_hi * 4 + z_lo), core: 2. Of those that a mesh axis runs over, the one named last changes fastest.
Arguments:
- latent: bfloat16 [16, 64, 1, 5, 16], P('tm', 'tile'), may hold values from -33 to 33
- proj_weight: bfloat16 [16, 256], replicated, may hold values from -1.5 to 1.5
- first_gain: float32 [256], replicated, may hold values from 0.1 to 1.9
- first_shift: float32 [256], replicated, may hold values from -0.5 to 0.5
- half_weight: bfloat16 [27, 256, 256], replicated, may hold values from -0.078125 to 0.078125
- second_gain: float32 [256], replicated, may hold values from 0.1 to 1.9
- second_shift: float32 [256], replicated, may hold values from -0.5 to 0.5
- full_weight: bfloat16 [27, 256, 128], P(None, None, 'tm'), may hold values from -0.078125 to 0.078125
- full_bias: float32 [128], replicated, may hold values from -0.5 to 0.5
- anchors: int32 [65], replicated, may hold values from 0 to 320, as said below
- reach: int32 [65], replicated, may hold values from 0 to 4, as said below
Outputs:
- decoded: bfloat16 [16, 64, 8, 40, 128], P('tm', 'tile')
Inputs may be any that keep to these rules, and one draw needn't show every extreme that they name: `anchors`: entry 0 is 0 and entry 64 is 320; entry j differs from j * 5 by at most 1, and both extremes occur in every draw. `reach`: entries 0 and 64 are 0; the others are 1 to 4; entry 1 is 4, and 1 occurs in every draw.
All inputs are finite; a program needn't handle non-finite values.
Results may differ from a plain program's by a relative error of at most 0.0055.
Values may be sent and summed in bfloat16 or wider, within the bound.
A program may use at most 64 MiB of HBM per device.

v0:
```python
import jax
import jax.numpy as jnp
from jax import lax
from jax.sharding import PartitionSpec as P

GROUPS = 32
MARGIN = 5


def copy_for_each(shard, axis):
    peers = lax.axis_size(axis)
    return lax.all_to_all(
        jnp.broadcast_to(shard[None], (peers, *shard.shape)), axis, 0, 0, tiled=True
    )


def of_everyone(shard, axis):
    everything = copy_for_each(shard, axis)
    return jnp.sum(everything, axis=0)


def padded(block, sides, width):
    for axis, dim in sides:
        count = lax.axis_size(axis)
        forward = [(i, i + 1) for i in range(count - 1)]
        backward = [(target, source) for source, target in forward]
        low = lax.ppermute(
            lax.slice_in_dim(block, block.shape[dim] - width, None, axis=dim), axis, forward
        )
        high = lax.ppermute(lax.slice_in_dim(block, 0, width, axis=dim), axis, backward)
        block = jnp.concatenate([low, block, high], axis=dim)
    return block


def from_behind(shard, axis, by):
    peers = lax.axis_size(axis)
    pairs = [(i, i + by) for i in range(peers) if 0 <= i + by < peers]
    return lax.ppermute(shard, axis, pairs)


def convolve(sequence, kernel_rows, row_pad):
    kernel = kernel_rows.reshape(3, 3, 3, kernel_rows.shape[1], kernel_rows.shape[2])
    result = lax.conv_general_dilated(
        sequence[None],
        kernel,
        (1, 1, 1),
        ((0, 0), (row_pad, row_pad), (1, 1)),
        dimension_numbers=("NDHWC", "DHWIO", "NDHWC"),
        preferred_element_type=jnp.float32,
    )
    return result[0]


def enlarge(values, factor):
    return jnp.repeat(jnp.repeat(values, factor, axis=1), factor, axis=2)


def moments(sums, squares, count):
    mean_value = sums / count
    variance = squares / count - mean_value * mean_value
    return (mean_value, lax.rsqrt(variance + 1e-06))


def normalize(values, mean_value, scale_value, gain, shift):
    return jax.nn.silu(gain * (values - mean_value) * scale_value + shift)


def blend_weight(tile_id, columns, anchors, reach):
    left_edge = 8 * anchors[tile_id]
    right_edge = 8 * anchors[tile_id + 1]
    left_reach = 8 * reach[tile_id]
    right_reach = 8 * reach[tile_id + 1]
    place = columns.astype(jnp.float32)
    rising = jnp.clip(
        (place - (left_edge - left_reach).astype(jnp.float32) + 0.5)
        / jnp.maximum(2 * left_reach, 1).astype(jnp.float32),
        0.0,
        1.0,
    )
    rising = jnp.where(left_reach > 0, rising, jnp.where(columns >= left_edge, 1.0, 0.0))
    falling = jnp.clip(
        ((right_edge + right_reach).astype(jnp.float32) - place - 0.5)
        / jnp.maximum(2 * right_reach, 1).astype(jnp.float32),
        0.0,
        1.0,
    )
    falling = jnp.where(right_reach > 0, falling, jnp.where(columns < right_edge, 1.0, 0.0))
    return jnp.minimum(rising, falling)


def group_sums(values, select, groups):
    masked = jnp.where(select, values, 0.0).reshape(-1, groups, values.shape[-1] // groups)
    return (jnp.sum(masked, axis=(0, 2)), jnp.sum(masked * masked, axis=(0, 2)))


def on_device(
    latent,
    proj_weight,
    first_gain,
    first_shift,
    half_weight,
    second_gain,
    second_shift,
    full_weight,
    full_bias,
    anchors,
    reach,
):
    column_tile = lax.axis_index("tile")
    tile_count = lax.axis_size("tile")
    time_index = lax.axis_index("tm")
    local = latent[:, 0]
    frame_count, row_count, col_count, latent_width = local.shape
    channels = proj_weight.shape[1]
    group_width = channels // GROUPS
    buffer_cols = col_count + 2 * MARGIN
    local_proj = jnp.dot(
        local.reshape(-1, latent_width), proj_weight, preferred_element_type=jnp.float32
    )
    first_sums = jax.tree.map(
        lambda part: of_everyone(part, "tile"), group_sums(local_proj, True, GROUPS)
    )
    first_mean, first_scale = moments(
        first_sums[0], first_sums[1], frame_count * row_count * col_count * tile_count * group_width
    )
    widened = padded(local, (("tile", 2),), MARGIN)
    projected = jnp.dot(
        widened.reshape(-1, latent_width), proj_weight, preferred_element_type=jnp.float32
    ).reshape(frame_count, row_count, buffer_cols, channels)
    lower_col = anchors[column_tile] - reach[column_tile]
    upper_col = anchors[column_tile + 1] + reach[column_tile + 1]
    coarse_cols = column_tile * col_count - MARGIN + jnp.arange(buffer_cols, dtype=jnp.int32)
    coarse_inside = (coarse_cols >= lower_col) & (coarse_cols < upper_col)
    first_norm = normalize(
        projected,
        jnp.repeat(first_mean, group_width),
        jnp.repeat(first_scale, group_width),
        first_gain,
        first_shift,
    )
    first_act = jnp.where(coarse_inside[:, None], first_norm, 0.0).astype(jnp.bfloat16)
    earlier = from_behind(first_act, "tm", 1)
    earlier = jnp.where(
        time_index == 0, jnp.concatenate([first_act[:1], first_act[:1]], 0), earlier
    )
    first_seq = enlarge(jnp.concatenate([earlier, first_act], 0), 4)
    middle = convolve(first_seq, half_weight, 1)
    fine_cols = 4 * (column_tile * col_count - MARGIN) + jnp.arange(
        4 * buffer_cols, dtype=jnp.int32
    )
    core_mask = (fine_cols >= 4 * anchors[column_tile]) & (fine_cols < 4 * anchors[column_tile + 1])
    second_sums = jax.tree.map(
        lambda part: of_everyone(part, "tile"), group_sums(middle, core_mask[:, None], GROUPS)
    )
    second_mean, second_scale = moments(
        second_sums[0],
        second_sums[1],
        frame_count * 16 * row_count * col_count * tile_count * group_width,
    )
    fine_inside = (fine_cols >= 4 * lower_col) & (fine_cols < 4 * upper_col)
    second_norm = normalize(
        middle,
        jnp.repeat(second_mean, group_width),
        jnp.repeat(second_scale, group_width),
        second_gain,
        second_shift,
    )
    second_act = jnp.where(fine_inside[:, None], second_norm, 0.0).astype(jnp.bfloat16)
    earlier_mid = from_behind(second_act[frame_count - 2 :], "tm", 1)
    earlier_mid = jnp.where(
        time_index == 0, jnp.concatenate([second_act[:1], second_act[:1]], 0), earlier_mid
    )
    second_seq = enlarge(jnp.concatenate([earlier_mid, second_act], 0), 2)
    whole_kernel = lax.all_gather(full_weight, "tm", axis=2, tiled=True)
    convolved = convolve(second_seq, whole_kernel, 1)
    tile_out = (convolved + full_bias).astype(jnp.bfloat16)
    span = 8 * MARGIN
    own_width = 8 * col_count
    out_cols = 8 * column_tile * col_count + jnp.arange(own_width, dtype=jnp.int32)
    has_left = (column_tile > 0).astype(jnp.float32)
    has_right = (column_tile < tile_count - 1).astype(jnp.float32)
    self_weight = blend_weight(column_tile, out_cols, anchors, reach)
    left_weight = blend_weight(jnp.maximum(column_tile - 1, 0), out_cols, anchors, reach) * has_left
    right_weight = (
        blend_weight(jnp.minimum(column_tile + 1, tile_count - 1), out_cols, anchors, reach)
        * has_right
    )
    denominator = self_weight + left_weight + right_weight
    edge_parts = jnp.concatenate([tile_out[:, :, :span], tile_out[:, :, span + own_width :]], 2)
    wide_rim = padded(edge_parts, (("tile", 2),), span)
    from_left = wide_rim[:, :, :span].astype(jnp.float32)
    from_right = wide_rim[:, :, 3 * span :].astype(jnp.float32)
    own_part = tile_out[:, :, span : span + own_width].astype(jnp.float32)
    left_full = jnp.pad(from_left, ((0, 0), (0, 0), (0, own_width - span), (0, 0)))
    right_full = jnp.pad(from_right, ((0, 0), (0, 0), (own_width - span, 0), (0, 0)))
    numerator = (
        self_weight[:, None] * own_part
        + left_weight[:, None] * left_full
        + right_weight[:, None] * right_full
    )
    result = (numerator / denominator[:, None]).astype(jnp.bfloat16)
    return result[:, None]


def solution(mesh):
    return jax.shard_map(
        on_device,
        mesh=mesh,
        in_specs=(
            P("tm", "tile", None, None, None),
            P(),
            P(),
            P(),
            P(),
            P(),
            P(),
            P(None, None, "tm"),
            P(),
            P(),
            P(),
        ),
        out_specs=P("tm", "tile", None, None, None),
        check_vma=False,
    )
```

profile of v0, /device:TPU:72, one launch (start us, length us, event | category | flops | bytes accessed | tf_op | source)
XLA Modules:
  0.0 202.9 jit_solution(4623958166468512287)
XLA Ops:
  6.5 1.4 copy.73
  8.0 3.4 %collective-permute-start = (bf16[2,1,5,16]{3,2,0,1:T(8,128)(2,1)}, bf16[2,1,5,16]{3,2,0,1:T(8,128)(2,1)}, u32[]{:S(2)}, u32[]{:S(2)}) collective-permute-start(bf16[2,1,5,16]{3,2,0,1:T(8,128)(2,1)} %bitcast.88), channel_id=1, source_target_pairs={{0,8},{8,16},{16,24},{24,32},{32,40},{40,48},{48,56},{56,64},{64,7... | collective-permute-start | bytes 968 | tf_op jit(solution)/shard_map/ppermute | solution.py:27
  11.4 10.6 %collective-permute-start.1 = (bf16[2,1,5,16]{3,2,0,1:T(8,128)(2,1)}, bf16[2,1,5,16]{3,2,0,1:T(8,128)(2,1)}, u32[]{:S(2)}, u32[]{:S(2)}) collective-permute-start(bf16[2,1,5,16]{3,2,0,1:T(8,128)(2,1)} %bitcast.88), channel_id=1, source_target_pairs={{8,0},{16,8},{24,16},{32,24},{40,32},{48,40},{56,48},{64,56},{72,6... | collective-permute-start | bytes 968 | tf_op jit(solution)/shard_map/ppermute | solution.py:30
  22.0 0.7 reshape.232
  22.7 1.4 copy.45
  24.1 1.1 fusion.61
  25.2 0.6 broadcast_in_dim.111
  25.8 13.7 %all-to-all-start = ((f32[64,1,32]{2,1,0:T(1,128)}), f32[64,1,32]{2,1,0:T(1,128)}, u32[]{:S(2)}, u32[]{:S(2)}) async-start(f32[64,1,32]{2,1,0:T(1,128)} %broadcast_in_dim.111), calls=%async_computation | async-start | bytes 65536 | tf_op jit(solution)/shard_map/all_to_all | solution.py:12
  39.6 0.7 all-gather.2.cloned.1.call-update
  40.3 1.6 fusion.66
  44.3 0.6 compare_and_fusion.1
  46.0 6.8 %all-to-all-done = f32[64,1,32]{2,1,0:T(1,128)} async-done(((f32[64,1,32]{2,1,0:T(1,128)}), f32[64,1,32]{2,1,0:T(1,128)}, u32[]{:S(2)}, u32[]{:S(2)}) %all-to-all-start) | async-done | bytes 8224 | tf_op jit(solution)/shard_map/all_to_all | solution.py:12
  52.8 0.6 broadcast_in_dim.113
  53.4 8.6 %all-to-all-start.1 = ((f32[64,1,32]{2,1,0:T(1,128)}), f32[64,1,32]{2,1,0:T(1,128)}, u32[]{:S(2)}, u32[]{:S(2)}) async-start(f32[64,1,32]{2,1,0:T(1,128)} %broadcast_in_dim.113), calls=%async_computation.1 | async-start | bytes 65536 | tf_op jit(solution)/shard_map/all_to_all | solution.py:12
  62.0 0.6 compare_and_fusion
  62.6 0.8 reduce_sum.87
  63.4 11.7 %all-to-all-done.1 = f32[64,1,32]{2,1,0:T(1,128)} async-done(((f32[64,1,32]{2,1,0:T(1,128)}), f32[64,1,32]{2,1,0:T(1,128)}, u32[]{:S(2)}, u32[]{:S(2)}) %all-to-all-start.1) | async-done | bytes 8224 | tf_op jit(solution)/shard_map/all_to_all | solution.py:12
  75.1 0.8 reduce_sum.89
  76.0 0.5 broadcast_multiply_fusion.1
  76.6 0.7 mul.256
  77.2 0.7 broadcast_in_dim.112
  77.9 0.7 sub.145
  78.6 0.9 select_convert_fusion.1
  79.5 1.9 collective-permute-start.2
  81.4 3.1 %collective-permute-done.2 = bf16[2,1,15,256]{3,2,0,1:T(8,128)(2,1)S(1)} collective-permute-done((bf16[2,1,15,256]{3,2,0,1:T(8,128)(2,1)S(1)}, bf16[2,1,15,256]{3,2,0,1:T(8,128)(2,1)S(1)}, u32[]{:S(2)}, u32[]{:S(2)}) %collective-permute-start.2) | collective-permute-done | bytes 15392 | tf_op jit(solution)/shard_map/ppermute | solution.py:38
  84.7 0.2 pad_bitcast_fusion
  85.1 2.0 convolution_select_fusion
  87.1 0.2 copy.72
  87.3 0.8 copy-done.1
  88.1 0.7 fusion.27
  88.8 0.8 reduce_sum.91
  89.6 0.7 reduce_sum.92
  90.2 1.3 broadcast_in_dim.121
  91.5 6.4 %all-to-all-start.2 = ((f32[64,1,32]{2,1,0:T(1,128)}), f32[64,1,32]{2,1,0:T(1,128)}, u32[]{:S(2)}, u32[]{:S(2)}) async-start(f32[64,1,32]{2,1,0:T(1,128)} %broadcast_in_dim.121), calls=%async_computation.2 | async-start | bytes 65536 | tf_op jit(solution)/shard_map/all_to_all | solution.py:12
  97.9 0.7 reduce_sum.95
  98.6 0.7 reduce_sum.96
  99.3 11.9 %all-to-all-done.2 = f32[64,1,32]{2,1,0:T(1,128)} async-done(((f32[64,1,32]{2,1,0:T(1,128)}), f32[64,1,32]{2,1,0:T(1,128)}, u32[]{:S(2)}, u32[]{:S(2)}) %all-to-all-start.2) | async-done | bytes 8224 | tf_op jit(solution)/shard_map/all_to_all | solution.py:12
  111.2 1.3 broadcast_in_dim.123
  112.5 6.2 %all-to-all-start.3 = ((f32[64,1,32]{2,1,0:T(1,128)}), f32[64,1,32]{2,1,0:T(1,128)}, u32[]{:S(2)}, u32[]{:S(2)}) async-start(f32[64,1,32]{2,1,0:T(1,128)} %broadcast_in_dim.123), calls=%async_computation.3 | async-start | bytes 65536 | tf_op jit(solution)/shard_map/all_to_all | solution.py:12
  118.8 0.5 compare_and_fusion.2
  119.3 0.8 reduce_sum.93
  120.1 12.0 %all-to-all-done.3 = f32[64,1,32]{2,1,0:T(1,128)} async-done(((f32[64,1,32]{2,1,0:T(1,128)}), f32[64,1,32]{2,1,0:T(1,128)}, u32[]{:S(2)}, u32[]{:S(2)}) %all-to-all-start.3) | async-done | bytes 8224 | tf_op jit(solution)/shard_map/all_to_all | solution.py:12
  132.1 0.8 reduce_sum.97
  133.0 0.5 broadcast_multiply_fusion
  133.6 0.7 mul.267
  134.2 0.7 broadcast_in_dim.122
  134.9 0.6 sub.149
  135.6 1.3 select_convert_fusion
  136.8 2.1 %collective-permute-start.3 = (bf16[2,4,60,256]{3,2,1,0:T(8,128)(2,1)S(1)}, bf16[2,4,60,256]{3,2,1,0:T(8,128)(2,1)S(1)}, u32[]{:S(2)}, u32[]{:S(2)}) collective-permute-start(bf16[2,4,60,256]{3,2,1,0:T(8,128)(2,1)S(1)} %select_convert_fusion), channel_id=1, source_target_pairs={{0,1},{1,2},{2,3},{3,4},{4,5},{5,6},{6,7},{8,9},{9,10},{10,11},{11... | collective-permute-start | bytes 737288 | tf_op jit(solution)/shard_map/ppermute | solution.py:38
  139.0 5.6 %collective-permute-done.3 = bf16[2,4,60,256]{3,2,1,0:T(8,128)(2,1)S(1)} collective-permute-done((bf16[2,4,60,256]{3,2,1,0:T(8,128)(2,1)S(1)}, bf16[2,4,60,256]{3,2,1,0:T(8,128)(2,1)S(1)}, u32[]{:S(2)}, u32[]{:S(2)}) %collective-permute-start.3) | collective-permute-done | bytes 245792 | tf_op jit(solution)/shard_map/ppermute | solution.py:38
  144.7 2.3 %broadcast_in_dim.127 = bf16[4,8,60,2,256]{4,3,2,1,0:T(2,128)(2,1)} broadcast(bf16[4,8,60,256]{3,2,1,0:T(8,128)(2,1)S(1)} %bitcast.93), dimensions={0,1,2,4} | broadcast | bytes 2949120 | tf_op jit(solution)/shard_map/broadcast_in_dim | solution.py:55
  147.1 5.2 %reshape.224 = bf16[4,8,1,120,256]{4,3,1,0,2:T(8,128)(2,1)} reshape(bf16[4,8,60,2,256]{4,3,2,1,0:T(2,128)(2,1)} %broadcast_in_dim.127) | data formatting | bytes 3932160 | tf_op jit(solution)/shard_map/broadcast_in_dim;reshape | solution.py:44
  152.3 2.8 %pad.2 = bf16[4,8,1,128,256]{4,3,1,0,2:T(8,128)(2,1)S(1)} pad(bf16[4,8,1,120,256]{4,3,1,0,2:T(8,128)(2,1)} %reshape.224, bf16[]{:T(256)} %constant.96), padding=0_0x0_0x0_0x1_7x0_0 | pad | bytes 4063234 | tf_op jit(solution)/shard_map/broadcast_in_dim;reshape | solution.py:44
  155.1 0.9 copy.57
  156.0 1.3 copy-done.2
  157.4 0.8 slice.34
  158.1 9.7 %fusion.9 = f32[2,8,8,16,128]{4,2,3,1,0:T(8,128)S(1)} fusion(bf16[3,3,3,256,128]{3,4,2,1,0:T(8,128)(2,1)} %bitcast.100, bf16[4,8,1,7,2,256]{5,3,4,1,0,2:T(8,128)(2,1)} %slice.34, bf16[4,8,1,8,16,256]{5,3,4,1,0,2:T(8,128)(2,1)} %copy-done.2, pred[8,16]{0,1:T(8,128)(4,1)S(1)} %copy-done.6), kind=kOutput, calls=%fused_computation.10 | convolution fusion | flops 3329228800 | bytes 5144704 | tf_op jit(solution)/shard_map/conv_general_dilated | solution.py:43
  167.8 0.2 copy.59
  168.0 0.5 copy-done.5
  168.6 0.8 copy-done.3
  169.3 0.8 fusion.65
  170.1 2.3 %collective-permute-start.4 = (bf16[2,8,40,128]{3,2,1,0:T(8,128)(2,1)}, bf16[2,8,40,128]{3,2,1,0:T(8,128)(2,1)}, u32[]{:S(2)}, u32[]{:S(2)}) collective-permute-start(bf16[2,8,40,128]{3,2,1,0:T(8,128)(2,1)} %get-tuple-element.13), channel_id=1, source_target_pairs={{0,8},{8,16},{16,24},{24,32},{32,40},{40,48},{48,56},{56,64},{64,7... | collective-permute-start | bytes 491528 | tf_op jit(solution)/shard_map/ppermute | solution.py:27
  172.4 10.4 %collective-permute-start.5 = (bf16[2,8,40,128]{3,2,1,0:T(8,128)(2,1)}, bf16[2,8,40,128]{3,2,1,0:T(8,128)(2,1)}, u32[]{:S(2)}, u32[]{:S(2)}) collective-permute-start(bf16[2,8,40,128]{3,2,1,0:T(8,128)(2,1)} %get-tuple-element.14), channel_id=1, source_target_pairs={{8,0},{16,8},{24,16},{32,24},{40,32},{48,40},{56,48},{64,56},{72,6... | collective-permute-start | bytes 491528 | tf_op jit(solution)/shard_map/ppermute | solution.py:30
  194.1 1.9 fusion.29
  (35 shorter events, 0.8 us)
Async XLA Ops:
  6.5 78.5 %copy-start = (bf16[27,256,256]{2,1,0:T(8,128)(2,1)S(1)}, bf16[27,256,256]{2,1,0:T(8,128)(2,1)}, u32[]{:S(2)}) copy-start(bf16[27,256,256]{2,1,0:T(8,128)(2,1)} %param.15) | copy-start | bytes 10616836
  8.0 70.6 %collective-permute-start = (bf16[2,1,5,16]{3,2,0,1:T(8,128)(2,1)}, bf16[2,1,5,16]{3,2,0,1:T(8,128)(2,1)}, u32[]{:S(2)}, u32[]{:S(2)}) collective-permute-start(bf16[2,1,5,16]{3,2,0,1:T(8,128)(2,1)} %bitcast.88), channel_id=1, source_target_pairs={{0,8},{8,16},{16,24},{24,32},{32,40},{40,48},{48,56},{56,64},{64,7... | collective-permute-start | bytes 968 | tf_op jit(solution)/shard_map/ppermute | solution.py:27
  11.4 67.2 %collective-permute-start.1 = (bf16[2,1,5,16]{3,2,0,1:T(8,128)(2,1)}, bf16[2,1,5,16]{3,2,0,1:T(8,128)(2,1)}, u32[]{:S(2)}, u32[]{:S(2)}) collective-permute-start(bf16[2,1,5,16]{3,2,0,1:T(8,128)(2,1)} %bitcast.88), channel_id=1, source_target_pairs={{8,0},{16,8},{24,16},{32,24},{40,32},{48,40},{56,48},{64,56},{72,6... | collective-permute-start | bytes 968 | tf_op jit(solution)/shard_map/ppermute | solution.py:30
  25.8 27.0 %all-to-all-start = ((f32[64,1,32]{2,1,0:T(1,128)}), f32[64,1,32]{2,1,0:T(1,128)}, u32[]{:S(2)}, u32[]{:S(2)}) async-start(f32[64,1,32]{2,1,0:T(1,128)} %broadcast_in_dim.111), calls=%async_computation | async-start | bytes 65536 | tf_op jit(solution)/shard_map/all_to_all | solution.py:12
  39.5 118.6 %all-gather.2.cloned.1.call-start = ((), (), s32[]{:S(2)}) async-start(), calls=%async_computation.4 | async-start | bytes 1990656 | tf_op jit(solution)/shard_map/all_gather | solution.py:174
  53.4 21.7 %all-to-all-start.1 = ((f32[64,1,32]{2,1,0:T(1,128)}), f32[64,1,32]{2,1,0:T(1,128)}, u32[]{:S(2)}, u32[]{:S(2)}) async-start(f32[64,1,32]{2,1,0:T(1,128)} %broadcast_in_dim.113), calls=%async_computation.1 | async-start | bytes 65536 | tf_op jit(solution)/shard_map/all_to_all | solution.py:12
  78.6 6.5 %copy-start.7 = (pred[8,8]{0,1:T(8,128)(4,1)S(1)}, pred[8,8]{0,1:T(8,128)(4,1)}, u32[]{:S(2)}) copy-start(pred[8,8]{0,1:T(8,128)(4,1)} %constant.105) | copy-start | bytes 196
  79.5 5.1 %collective-permute-start.2 = (bf16[2,1,15,256]{3,2,0,1:T(8,128)(2,1)S(1)}, bf16[2,1,15,256]{3,2,0,1:T(8,128)(2,1)S(1)}, u32[]{:S(2)}, u32[]{:S(2)}) collective-permute-start(bf16[2,1,15,256]{3,2,0,1:T(8,128)(2,1)S(1)} %bitcast.97), channel_id=1, source_target_pairs={{0,1},{1,2},{2,3},{3,4},{4,5},{5,6},{6,7},{8,9},{9,10},{10,11},{11... | collective-permute-start | bytes 46088 | tf_op jit(solution)/shard_map/ppermute | solution.py:38
  85.1 3.0 %copy-start.4 = (pred[60]{0:T(512)(128)(4,1)S(1)}, pred[60]{0:T(512)(128)(4,1)}, u32[]{:S(2)}) copy-start(pred[60]{0:T(512)(128)(4,1)} %compare_and_fusion) | copy-start | bytes 184
  87.3 0.8 copy-start.1
  91.5 19.7 %all-to-all-start.2 = ((f32[64,1,32]{2,1,0:T(1,128)}), f32[64,1,32]{2,1,0:T(1,128)}, u32[]{:S(2)}, u32[]{:S(2)}) async-start(f32[64,1,32]{2,1,0:T(1,128)} %broadcast_in_dim.121), calls=%async_computation.2 | async-start | bytes 65536 | tf_op jit(solution)/shard_map/all_to_all | solution.py:12
  112.5 19.6 %all-to-all-start.3 = ((f32[64,1,32]{2,1,0:T(1,128)}), f32[64,1,32]{2,1,0:T(1,128)}, u32[]{:S(2)}, u32[]{:S(2)}) async-start(f32[64,1,32]{2,1,0:T(1,128)} %broadcast_in_dim.123), calls=%async_computation.3 | async-start | bytes 65536 | tf_op jit(solution)/shard_map/all_to_all | solution.py:12
  136.8 7.7 %collective-permute-start.3 = (bf16[2,4,60,256]{3,2,1,0:T(8,128)(2,1)S(1)}, bf16[2,4,60,256]{3,2,1,0:T(8,128)(2,1)S(1)}, u32[]{:S(2)}, u32[]{:S(2)}) collective-permute-start(bf16[2,4,60,256]{3,2,1,0:T(8,128)(2,1)S(1)} %select_convert_fusion), channel_id=1, source_target_pairs={{0,1},{1,2},{2,3},{3,4},{4,5},{5,6},{6,7},{8,9},{9,10},{10,11},{11... | collective-permute-start | bytes 737288 | tf_op jit(solution)/shard_map/ppermute | solution.py:38
  155.1 3.1 %copy-start.6 = (pred[8,16]{0,1:T(8,128)(4,1)S(1)}, pred[8,16]{0,1:T(8,128)(4,1)}, u32[]{:S(2)}) copy-start(pred[8,16]{0,1:T(8,128)(4,1)} %constant.104) | copy-start | bytes 388
  156.0 1.3 copy-start.2
  167.8 0.7 copy-start.5
  168.6 0.8 copy-start.3
  170.1 24.0 %collective-permute-start.4 = (bf16[2,8,40,128]{3,2,1,0:T(8,128)(2,1)}, bf16[2,8,40,128]{3,2,1,0:T(8,128)(2,1)}, u32[]{:S(2)}, u32[]{:S(2)}) collective-permute-start(bf16[2,8,40,128]{3,2,1,0:T(8,128)(2,1)} %get-tuple-element.13), channel_id=1, source_target_pairs={{0,8},{8,16},{16,24},{24,32},{32,40},{40,48},{48,56},{56,64},{64,7... | collective-permute-start | bytes 491528 | tf_op jit(solution)/shard_map/ppermute | solution.py:27
  172.4 21.7 %collective-permute-start.5 = (bf16[2,8,40,128]{3,2,1,0:T(8,128)(2,1)}, bf16[2,8,40,128]{3,2,1,0:T(8,128)(2,1)}, u32[]{:S(2)}, u32[]{:S(2)}) collective-permute-start(bf16[2,8,40,128]{3,2,1,0:T(8,128)(2,1)} %get-tuple-element.14), channel_id=1, source_target_pairs={{8,0},{16,8},{24,16},{32,24},{40,32},{48,40},{56,48},{64,56},{72,6... | collective-permute-start | bytes 491528 | tf_op jit(solution)/shard_map/ppermute | solution.py:30
Sparse Core Ops, SparseCore 0:
  42.4 39.0 all-gather.1
where the time goes:
time: 204 us; the launch traced here: 203 us
  starting transfers between devices  65.7 us (32%)
  waiting for transfers between devices  51.8 us (25%)
  local copies, waits for them, and re-layouts  31.7 us (16%)
  between operations  28.5 us (14%)
  matrix products  13.6 us (7%)
  other arithmetic  11.6 us (6%)
    all_to_all x4, waiting for transfers between devices, copy_for_each(): lax.all_to_all(jnp.broadcast_to(shard[None], (peers, *shard.shape)), axis...  42.4 us
    all_to_all x4, starting transfers between devices, copy_for_each(): lax.all_to_all(jnp.broadcast_to(shard[None], (peers, *shard.shape)), axis...  34.8 us
    ppermute x2, starting transfers between devices, padded(): lax.ppermute(lax.slice_in_dim(block, 0, width, axis=dim), axis, backward)  21.1 us
    conv_general_dilated x2, matrix products, convolve(): lax.conv_general_dilated(sequence[None], kernel, (1, 1, 1), ((0, 0), (row...  11.7 us
    ppermute x2, waiting for transfers between devices, from_behind(): return lax.ppermute(shard, axis, pairs)  8.68 us
    another operation x2, local copies, waits for them, and re-layouts, convolve(): sequence[None]  7.99 us
    ppermute x2, starting transfers between devices, padded(): lax.ppermute(lax.slice_in_dim(block, block.shape[dim] - width, None, axis...  5.7 us
    unnamed x17, local copies, waits for them, and re-layouts  4.78 us
  transfers between devices with their start and end apart: 11, of which 6 were waited for; matrix products, arithmetic and copies ran while one was open for 19% of the time, Pallas kernels for 0%

commit v1 on v0

v1 whole, which is shorter than its diff:
```python
import jax
import jax.numpy as jnp
from jax import lax
from jax.experimental import pallas as pl
from jax.experimental.pallas import tpu as pltpu
from jax.sharding import PartitionSpec as P

GROUPS = 32
NX, NZH, NY, NT = 4, 2, 8, 8
TILES = NX * NZH * NY
LCW = 5
BF = jnp.bfloat16
F32 = jnp.float32
MESH = pl.DeviceIdType.MESH

COMBOS = ("01", "12", "0", "2", "012")
ROW_USES = {
    "01": ((0, 1), (1, 5), (2, 7)),
    "12": ((0, 0), (1, 2), (2, 6)),
    "0": ((0, 2), (1, 6)),
    "2": ((1, 1), (2, 5)),
    "012": ((1, 3),),
}
COL_USES = {
    "01": ((0, 1, 0), (1, 5, 0), (2, 7, 0)),
    "12": ((0, 0, 0), (1, 2, 0), (2, 6, 0)),
    "0": ((0, 2, 0), (1, 6, 0), (2, 0, 1)),
    "2": ((0, 7, -1), (1, 1, 0), (2, 5, 0)),
    "012": ((1, 3, 0),),
}
SLOT = {0: 0, 1: 1, 2: 2, 3: 3, 4: 3, 5: 4, 6: 5, 7: 6}


def dot(a, b):
    return jnp.dot(a, b, preferred_element_type=F32)


def exact_dot(x, ones):
    high = x.astype(BF)
    rest = x - high.astype(F32)
    middle = rest.astype(BF)
    low = (rest - middle.astype(F32)).astype(BF)
    return dot(high, ones) + dot(middle, ones) + dot(low, ones)


def iota(shape, dim):
    return lax.broadcasted_iota(jnp.int32, shape, dim)


def encode(sums, squares):
    channel, lane = iota((256, 128), 0), iota((256, 128), 1)
    ones = jnp.where(((channel >> 3) == (lane & 31)) & (lane < 64), 1.0, 0.0).astype(BF)
    row = iota((8, 256), 0)
    stacked = jnp.where(row == 0, sums, jnp.where(row == 1, squares, 0.0))
    coded = exact_dot(stacked, ones)
    return jnp.where(iota((1, 128), 1) < 32, coded[0:1], coded[1:2])


def decode(totals, count):
    lane, channel = iota((128, 256), 0), iota((128, 256), 1)
    ones = jnp.where(((channel >> 3) == (lane & 31)) & (lane < 64), 1.0, 0.0).astype(BF)
    row, place = iota((8, 128), 0), iota((8, 128), 1)
    stacked = jnp.zeros((8, 128), F32)
    for i, total in enumerate(totals):
        stacked = jnp.where((row == 2 * i) & (place < 32), total, stacked)
        stacked = jnp.where((row == 2 * i + 1) & (place >= 32), total, stacked)
    wide = exact_dot(stacked, ones)
    result = []
    for i in range(len(totals)):
        mean = wide[2 * i : 2 * i + 1] / count
        variance = wide[2 * i + 1 : 2 * i + 2] / count - mean * mean
        result.append((mean, lax.rsqrt(variance + 1e-06)))
    return result


def normalize(values, mean, scale, gain, shift):
    v = gain * (values - mean) * scale + shift
    half = 0.5 * v
    return half + half * jnp.tanh(half)


def tile_at(y, z, x):
    return y * (NZH * NX) + z * NX + x


def around(j, k):
    other = j + k
    return jnp.clip(other, 0, TILES - 1), (other >= 0) & (other < TILES)


def front_kernel(
    lat_hbm, wp_hbm, gain_hbm, shift_hbm, hw_hbm, fw_hbm, anchors_hbm, reach_hbm,
    mid_ref, moments_ref, wc_ref,
    lbuf, wp, gain, shift, hw, wt, anchors, reach, fl, a1, b1, a2, b2,
    local_sem, sa1, ra1, sb1, rb1, sa2, ra2, sb2, rb2, sl, rl, sw, rw, ss, rs,
):
    j = lax.axis_index("tile")
    tm = lax.axis_index("tm")
    y, z, x = j // (NZH * NX), (j // NX) % NZH, j % NX
    zl = tm // 2

    loads = [
        pltpu.make_async_copy(src, dst, local_sem.at[i])
        for i, (src, dst) in enumerate(
            (
                (lat_hbm, lbuf.at[0, pl.ds(1, LCW)]),
                (wp_hbm, wp),
                (fw_hbm, wt.at[tm]),
                (anchors_hbm, anchors),
                (reach_hbm, reach),
                (gain_hbm, gain),
                (shift_hbm, shift),
                (hw_hbm.at[pl.ds(0, 9)], hw.at[pl.ds(0, 9)]),
                (hw_hbm.at[pl.ds(9, 9)], hw.at[pl.ds(9, 9)]),
                (hw_hbm.at[pl.ds(18, 9)], hw.at[pl.ds(18, 9)]),
            )
        )
    ]
    for load in loads:
        load.start()

    column = [(tile_at((y + d) % NY, z, x), tm) for d in range(NY)]
    plane = [(s, dz, dx) for s in range(3) for dz in range(NZH) for dx in range(NX)][1:]

    def plane_at(sign, s, dz, dx):
        return (
            tile_at(y, (z + dz) % NZH, (x + sign * dx + NX) % NX),
            (tm + sign * s + NT) % NT,
        )

    def chip_at(step):
        far = (zl + step + 4) // 4
        return (tile_at(y, (z + far + 1) % NZH, x), (tm + 2 * step + NT) % NT)

    sibling = (j, tm + 1 - 2 * (tm % 2))
    chips = [chip_at(1), chip_at(-1), chip_at(2), chip_at(-2)]

    barrier = pltpu.get_barrier_semaphore()
    greeted = column[1:] + [plane_at(-1, *p) for p in plane] + chips + [sibling]
    for s in range(3):
        greeted.append(((j + 1) % TILES, (tm - s + NT) % NT))
        greeted.append(((j + TILES - 1) % TILES, (tm - s + NT) % NT))
    for peer in greeted:
        pl.semaphore_signal(barrier, inc=1, device_id=peer, device_id_type=MESH)

    fl[...] = jnp.zeros_like(fl)
    loads[0].wait()
    loads[1].wait()
    for c in range(LCW):
        fl[pl.ds(32 + 1 + c, 2, stride=8), :] = lbuf[0, 1 + c].astype(F32)
    own = dot(fl[32:48].astype(BF), wp[...])
    a1[0] = encode(jnp.sum(own, axis=0, keepdims=True), jnp.sum(own * own, axis=0, keepdims=True))

    pl.semaphore_wait(barrier, len(greeted))

    def send(src, dst, send_sem, recv_sem, peer):
        copy = pltpu.make_async_remote_copy(
            src_ref=src, dst_ref=dst, send_sem=send_sem, recv_sem=recv_sem,
            device_id=peer, device_id_type=MESH,
        )
        copy.start()
        return copy

    def send_column(buf, s_sem, r_sem):
        return [send(buf.at[0], buf.at[d], s_sem.at[d], r_sem.at[d], column[d]) for d in range(1, NY)]

    def send_plane(buf, s_sem, r_sem, shifts):
        copies = []
        for s, dz, dx in plane:
            if s < shifts:
                i = s * 8 + dz * NX + dx
                copies.append(
                    send(buf.at[0], buf.at[i], s_sem.at[i], r_sem.at[i], plane_at(1, s, dz, dx))
                )
        return copies

    sent = []
    first_column = send_column(a1, sa1, ra1)
    lat_copies = []
    for s in range(3):
        for i, (src, dst, tile) in enumerate(
            (
                (lbuf.at[0, LCW], lbuf.at[s, 0], (j + 1) % TILES),
                (lbuf.at[0, 1], lbuf.at[s, LCW + 1], (j + TILES - 1) % TILES),
                (lbuf.at[0, pl.ds(1, LCW)], lbuf.at[s, pl.ds(1, LCW)], j),
            )
        ):
            if i == 2 and s == 0:
                continue
            n = 3 * s + i
            lat_copies.append(send(src, dst, sl.at[n], rl.at[n], (tile, (tm + s) % NT)))
    loads[2].wait()
    sibling_copies = [send(wt.at[tm], wt.at[tm], ss.at[0], rs.at[0], sibling)]

    for copy in first_column:
        copy.wait_recv()
    b1[0] = jnp.sum(a1[...], axis=0)
    first_plane = send_plane(b1, sb1, rb1, 3)

    half = 14
    chip_copies = [
        send(wt.at[tm], wt.at[tm], sw.at[0], rw.at[0], chips[0]),
        send(wt.at[tm], wt.at[tm], sw.at[1], rw.at[1], chips[1]),
        send(wt.at[tm, pl.ds(0, half)], wt.at[tm, pl.ds(0, half)], sw.at[2], rw.at[2], chips[2]),
        send(
            wt.at[tm, pl.ds(half, 27 - half)], wt.at[tm, pl.ds(half, 27 - half)],
            sw.at[3], rw.at[3], chips[3],
        ),
    ]

    for copy in lat_copies:
        copy.wait_recv()
    for s in range(3):
        for c in range(LCW + 2):
            fl[pl.ds(16 * (2 - s) + c, 2, stride=8), :] = lbuf[s, c].astype(F32)
    projected = dot(fl[...].astype(BF), wp[...])
    for load in loads[3:]:
        load.wait()

    for copy in first_plane:
        copy.wait_recv()
    totals = [jnp.sum(b1[8 * s : 8 * s + 8], axis=0) for s in range(3)]
    stats = decode(totals, float(2 * LCW * TILES * 8))
    frames = []
    for s in (2, 1, 0):
        block = normalize(
            projected[16 * (2 - s) : 16 * (2 - s) + 16], stats[s][0], stats[s][1], gain[...], shift[...]
        )
        frames += [block[0:8], block[8:16]]
    frames[2] = jnp.where(tm == 0, frames[4], frames[2])
    frames[3] = jnp.where(tm == 0, frames[4], frames[3])
    frames[0] = jnp.where(tm == 1, frames[2], frames[0])
    frames[1] = jnp.where(tm == 1, frames[2], frames[1])
    seqs = [jnp.concatenate(frames[a : a + 4], axis=0).astype(BF) for a in range(3)]

    col = 5 * j - 1 + (iota((32, 256), 0) & 7)
    local_col = iota((32, 256), 0) & 7
    masks, cores = [], []
    for k in (-1, 0, 1):
        t, there = around(j, k)
        low, high = anchors[t], anchors[t + 1]
        inside = (col >= low - reach[t]) & (col < high + reach[t + 1])
        masks.append(jnp.where(inside, 1.0, 0.0))
        there = jnp.where(there, 1, 0)
        core = (col >= low) & (col < high) & (local_col >= 1) & (local_col <= LCW)
        cores.append(jnp.where(core, there.astype(F32), 0.0))

    taps = [
        [
            dot(seqs[0], hw[3 * b + d]) + dot(seqs[1], hw[9 + 3 * b + d]) + dot(seqs[2], hw[18 + 3 * b + d])
            for d in range(3)
        ]
        for b in range(3)
    ]
    sums = jnp.zeros((8, 256), F32)
    squares = jnp.zeros((8, 256), F32)

    def rolled(v, by):
        return pltpu.roll(v.reshape(4, 8, 256), by % 8, 1).reshape(32, 256)

    for r in range(3):
        if r == 0:
            q = [taps[1][d] + taps[2][d] for d in range(3)]
        elif r == 1:
            q = [taps[0][d] + taps[1][d] + taps[2][d] for d in range(3)]
        else:
            q = [taps[0][d] + taps[1][d] for d in range(3)]
        right = q[1] + q[2]
        left = q[0] + q[1]
        whole = left + q[2]
        for k in range(3):
            m = masks[k]
            kinds = (
                rolled(m * q[0], 1) + m * right,
                m * whole,
                m * left + rolled(m * q[2], -1),
            )
            for p in range(3):
                mid_ref[k * 9 + r * 3 + p] = kinds[p]
                times = (2.0 if r == 1 else 1.0) * (2.0 if p == 1 else 1.0)
                part = cores[k][16:32] * kinds[p][16:32]
                square = part * kinds[p][16:32]
                sums = sums + times * (part[0:8] + part[8:16])
                squares = squares + times * (square[0:8] + square[8:16])
    a2[0] = encode(jnp.sum(sums, axis=0, keepdims=True), jnp.sum(squares, axis=0, keepdims=True))
    second_column = send_column(a2, sa2, ra2)

    for copy in chip_copies:
        copy.wait_recv()
    for i, shard in enumerate(((tm + 2) % NT, (tm + 4) % NT, (tm + 6) % NT)):
        sibling_copies.append(
            send(wt.at[shard], wt.at[shard], ss.at[1 + i], rs.at[1 + i], sibling)
        )

    for copy in second_column:
        copy.wait_recv()
    b2[0] = jnp.sum(a2[...], axis=0)
    second_plane = send_plane(b2, sb2, rb2, 2)

    for copy in sibling_copies:
        copy.wait_recv()

    def combine(i, carry):
        a, n = i // NT, i % NT
        w = [[wt[n, 9 * a + 3 * b + d].astype(F32) for d in range(3)] for b in range(3)]

        def combos(u):
            first = u[0] + u[1]
            return {"0": u[0], "2": u[2], "01": first, "12": u[1] + u[2], "012": first + u[2]}

        by_col = [combos([w[b][d] for b in range(3)]) for d in range(3)]
        for rc, row_class in enumerate(COMBOS):
            both = combos([by_col[d][row_class] for d in range(3)])
            for cc, col_class in enumerate(COMBOS):
                wc_ref[
                    rc,
                    pl.ds(pl.multiple_of(cc * 128 + n * 16, 16), 16),
                    pl.ds(pl.multiple_of(a * 256, 256), 256),
                ] = both[col_class].astype(BF)
        return carry

    lax.fori_loop(0, 3 * NT, combine, 0)

    for copy in second_plane:
        copy.wait_recv()
    totals = [jnp.sum(b2[8 * s : 8 * s + 8], axis=0) for s in range(2)]
    stats = decode(totals, float(2 * 16 * LCW * TILES * 8))
    moments_ref[0:1] = stats[1][0]
    moments_ref[1:2] = stats[1][1]
    moments_ref[2:3] = stats[0][0]
    moments_ref[3:4] = stats[0][1]
    for copy in (
        first_column + lat_copies + first_plane + chip_copies + second_column + sibling_copies + second_plane
    ):
        copy.wait_send()


def blend_weight(columns, low, high, low_reach, high_reach):
    left_edge, right_edge = 8 * low, 8 * high
    left_reach, right_reach = 8 * low_reach, 8 * high_reach
    place = columns.astype(F32)
    rising = jnp.clip(
        (place - (left_edge - left_reach).astype(F32) + 0.5)
        / jnp.maximum(2 * left_reach, 1).astype(F32),
        0.0,
        1.0,
    )
    rising = jnp.where(left_reach > 0, rising, jnp.where(columns >= left_edge, 1.0, 0.0))
    falling = jnp.clip(
        ((right_edge + right_reach).astype(F32) - place - 0.5)
        / jnp.maximum(2 * right_reach, 1).astype(F32),
        0.0,
        1.0,
    )
    falling = jnp.where(right_reach > 0, falling, jnp.where(columns < right_edge, 1.0, 0.0))
    return jnp.minimum(rising, falling)


def back_kernel(
    mid, moments, wc, gain, shift, bias, anchors, reach, out_ref, xs, acc, rows
):
    j = lax.axis_index("tile")
    tm = lax.axis_index("tm")
    col = 5 * j - 1 + (iota((16, 256), 0) & 7)
    for k in range(3):
        t, _ = around(j, k - 1)
        inside = (col >= anchors[t] - reach[t]) & (col < anchors[t + 1] + reach[t + 1])
        for r in range(3):
            for p in range(3):
                values = mid[k * 9 + r * 3 + p]
                before = normalize(values[0:16], moments[0:1], moments[1:2], gain[...], shift[...])
                now = normalize(values[16:32], moments[2:3], moments[3:4], gain[...], shift[...])
                now = jnp.where(inside, now, 0.0)
                before = jnp.where(inside, before, 0.0)
                first = jnp.concatenate([now[0:8], now[0:8]], axis=0)
                before = jnp.where(tm == 0, first, before)
                at = (r * 3 + p) * 48 + k * 16
                xs[at : at + 16, 0:256] = before.astype(BF)
                xs[at : at + 16, 256:512] = jnp.concatenate([before[8:16], now[0:8]], axis=0).astype(BF)
                xs[at : at + 16, 512:768] = now.astype(BF)

    seen = set()
    for rc, row_class in enumerate(COMBOS):
        uses = ROW_USES[row_class]
        r0, r1 = uses[0][0], uses[-1][0] + 1
        for pair in ((0, 1), (2, 3), (4,)):
            if pair == (4,):
                lhs = [xs[r * 144 + 48 : r * 144 + 96] for r in range(r0, r1)]
                lhs = lhs[0] if len(lhs) == 1 else jnp.concatenate(lhs, axis=0)
                inputs = (1,)
            else:
                lhs = xs[r0 * 144 : r1 * 144]
                inputs = (0, 1, 2)
            rhs = wc[rc, pair[0] * 128 : (pair[-1] + 1) * 128]
            result = lax.dot_general(
                lhs, rhs, (((1,), (1,)), ((), ())), preferred_element_type=F32
            )
            for r, big_row in uses:
                for half, cc in enumerate(pair):
                    for p, big_col, by in COL_USES[COMBOS[cc]]:
                        at = ((r - r0) * len(inputs) + inputs.index(p)) * 48
                        part = result[at : at + 48, half * 128 : half * 128 + 128]
                        if by:
                            part = pltpu.roll(part.reshape(6, 8, 128), by % 8, 1).reshape(48, 128)
                        slot = SLOT[big_row] * 7 + SLOT[big_col]
                        if slot in seen:
                            acc[slot] += part
                        else:
                            seen.add(slot)
                            acc[slot] = part

    weights = []
    for c in range(8):
        columns = 40 * j - 8 + 8 * iota((8, 128), 0) + c
        parts = []
        for k in range(3):
            t, there = around(j, k - 1)
            weight = blend_weight(columns, anchors[t], anchors[t + 1], reach[t], reach[t + 1])
            parts.append(weight * jnp.where(there, 1, 0).astype(F32))
        total = parts[0] + parts[1] + parts[2]
        keep = (iota((8, 128), 0) >= 1) & (iota((8, 128), 0) <= LCW)
        total = jnp.where(keep, total, 1.0)
        weights.append([part / total for part in parts])

    for t in range(2):
        for big_row in (0, 1, 2, 3, 5, 6, 7):
            for c in range(8):
                slot = SLOT[big_row] * 7 + SLOT[c]
                value = None
                for k in range(3):
                    at = k * 16 + t * 8
                    piece = (acc[slot, at : at + 8] + bias[...]).astype(BF).astype(F32) * weights[c][k]
                    value = piece if value is None else value + piece
                rows[pl.ds(c, 8, stride=8), :] = value
            final = rows[8:48].astype(BF)
            out_ref[t, big_row] = final
            if big_row == 3:
                out_ref[t, 4] = final


def on_device(
    latent,
    proj_weight,
    first_gain,
    first_shift,
    half_weight,
    second_gain,
    second_shift,
    full_weight,
    full_bias,
    anchors,
    reach,
):
    lat = latent.transpose(1, 2, 3, 0, 4).reshape(LCW, 2, 16)
    shard = full_weight.transpose(0, 2, 1)
    any_space = pl.BlockSpec(memory_space=pl.ANY)
    vmem = pl.BlockSpec(memory_space=pltpu.VMEM)
    smem = pl.BlockSpec(memory_space=pltpu.SMEM)
    dma = pltpu.SemaphoreType.DMA
    mid, moments, wc = pl.pallas_call(
        front_kernel,
        name="front",
        out_shape=(
            jax.ShapeDtypeStruct((27, 32, 256), F32),
            jax.ShapeDtypeStruct((8, 256), F32),
            jax.ShapeDtypeStruct((5, 640, 768), BF),
        ),
        in_specs=[any_space] * 8,
        out_specs=(vmem, vmem, vmem),
        scratch_shapes=[
            pltpu.VMEM((3, LCW + 2, 2, 16), BF),
            pltpu.VMEM((16, 256), BF),
            pltpu.VMEM((1, 256), F32),
            pltpu.VMEM((1, 256), F32),
            pltpu.VMEM((27, 256, 256), BF),
            pltpu.VMEM((NT, 27, 16, 256), BF),
            pltpu.SMEM((TILES + 1,), jnp.int32),
            pltpu.SMEM((TILES + 1,), jnp.int32),
            pltpu.VMEM((48, 16), F32),
            pltpu.VMEM((8, 1, 128), F32),
            pltpu.VMEM((24, 1, 128), F32),
            pltpu.VMEM((8, 1, 128), F32),
            pltpu.VMEM((16, 1, 128), F32),
            dma((10,)),
            dma((8,)), dma((8,)), dma((24,)), dma((24,)),
            dma((8,)), dma((8,)), dma((16,)), dma((16,)),
            dma((9,)), dma((9,)), dma((4,)), dma((4,)), dma((4,)), dma((4,)),
        ],
        compiler_params=pltpu.CompilerParams(
            collective_id=0, has_side_effects=True, vmem_limit_bytes=20 * 2**20
        ),
    )(
        lat, proj_weight, first_gain.reshape(1, 256), first_shift.reshape(1, 256),
        half_weight, shard, anchors, reach,
    )
    out = pl.pallas_call(
        back_kernel,
        name="back",
        out_shape=jax.ShapeDtypeStruct((2, 8, 8 * LCW, 128), BF),
        in_specs=[vmem] * 6 + [smem] * 2,
        out_specs=vmem,
        scratch_shapes=[
            pltpu.VMEM((432, 768), BF),
            pltpu.VMEM((49, 48, 128), F32),
            pltpu.VMEM((64, 128), F32),
        ],
        compiler_params=pltpu.CompilerParams(vmem_limit_bytes=20 * 2**20),
    )(
        mid, moments, wc, second_gain.reshape(1, 256), second_shift.reshape(1, 256),
        full_bias.reshape(1, 128), anchors, reach,
    )
    return out[:, None]


def solution(mesh):
    return jax.shard_map(
        on_device,
        mesh=mesh,
        in_specs=(
            P("tm", "tile", None, None, None),
            P(),
            P(),
            P(),
            P(),
            P(),
            P(),
            P(None, None, "tm"),
            P(),
            P(),
            P(),
        ),
        out_specs=P("tm", "tile", None, None, None),
        check_vma=False,
    )
```

time: 204 us -> 54 us (0.26)
  the two profiles are of different devices: /device:TPU:72 before, /device:TPU:1 now
where the time goes in v1:
time: 54 us; the launch traced here: 53.7 us
  Pallas kernels  44.7 us (83%)
  local copies, waits for them, and re-layouts  8.99 us (17%)
    pallas_call x1, Pallas kernels, on_device(): pl.pallas_call(front_kernel, name='front', out_shape=(jax.ShapeDtypeStruc...  41.2 us
    unnamed x22, local copies, waits for them, and re-layouts  8.99 us
    pallas_call x1, Pallas kernels, on_device(): pl.pallas_call(back_kernel, name='back', out_shape=jax.ShapeDtypeStruct((...  3.41 us

profile of v1, /device:TPU:1, one launch (start us, length us, event | category | flops | bytes accessed | tf_op | source)
XLA Modules:
  0.0 53.7 jit_solution(5177526458944704489)
XLA Ops:
  0.0 0.0 copy-start
  0.0 2.0 %copy-done = bf16[27,256,256]{2,1,0:T(8,128)(2,1)S(1)} copy-done((bf16[27,256,256]{2,1,0:T(8,128)(2,1)S(1)}, bf16[27,256,256]{2,1,0:T(8,128)(2,1)}, u32[]{:S(2)}) %copy-start) | copy-done | bytes 3538968
  2.0 0.0 copy-start.1
  2.0 0.9 %copy-done.1 = bf16[27,256,16]{1,2,0:T(8,128)(2,1)S(1)} copy-done((bf16[27,256,16]{1,2,0:T(8,128)(2,1)S(1)}, bf16[27,256,16]{1,2,0:T(8,128)(2,1)}, u32[]{:S(2)}) %copy-start.1) | copy-done | bytes 221208
  2.9 0.0 copy-start.2
  2.9 0.7 %copy-done.2 = bf16[16,256]{1,0:T(8,128)(2,1)S(1)} copy-done((bf16[16,256]{1,0:T(8,128)(2,1)S(1)}, bf16[16,256]{1,0:T(8,128)(2,1)}, u32[]{:S(2)}) %copy-start.2) | copy-done | bytes 8216
  3.6 0.0 copy-start.3
  3.6 0.7 %copy-done.3 = bf16[2,1,1,5,16]{4,0,3,2,1:T(2,128)(2,1)S(1)} copy-done((bf16[2,1,1,5,16]{4,0,3,2,1:T(2,128)(2,1)S(1)}, bf16[2,1,1,5,16]{4,0,3,2,1:T(2,128)(2,1)}, u32[]{:S(2)}) %copy-start.3) | copy-done | bytes 344
  4.3 0.0 copy-start.4
  4.3 0.7 %copy-done.4 = s32[65]{0:T(128)S(1)} copy-done((s32[65]{0:T(128)S(1)}, s32[65]{0:T(128)}, u32[]{:S(2)}) %copy-start.4) | copy-done | bytes 284
  5.0 0.0 copy-start.5
  5.0 0.7 %copy-done.5 = s32[65]{0:T(128)S(1)} copy-done((s32[65]{0:T(128)S(1)}, s32[65]{0:T(128)}, u32[]{:S(2)}) %copy-start.5) | copy-done | bytes 284
  5.6 0.0 copy-start.8
  5.6 0.7 %copy-done.8 = f32[256]{0:T(256)S(1)} copy-done((f32[256]{0:T(256)S(1)}, f32[256]{0:T(256)}, u32[]{:S(2)}) %copy-start.8) | copy-done | bytes 1048
  6.3 0.0 copy-start.9
  6.3 0.7 %copy-done.9 = f32[256]{0:T(256)S(1)} copy-done((f32[256]{0:T(256)S(1)}, f32[256]{0:T(256)}, u32[]{:S(2)}) %copy-start.9) | copy-done | bytes 1048
  7.0 41.2 %front.1 = (f32[27,32,256]{2,1,0:T(8,128)S(1)}, f32[8,256]{1,0:T(8,128)S(1)}, bf16[5,640,768]{2,1,0:T(8,128)(2,1)S(1)}) custom-call(bf16[5,2,16]{2,1,0:T(2,128)(2,1)S(1)} %bitcast.13, bf16[16,256]{1,0:T(8,128)(2,1)S(1)} %copy-done.2, f32[1,256]{1,0:T(1,128)S(1)} %bitcast.16, f32[1,256]{1,0:T(1,128)S(1)} %bitcast.17, bf16[27,256,256]{2,1,0:T(8,128)(2,1)S(1)} %copy-done, ...), custom_call_target="tpu_custom_call" | custom-call | tf_op jit(solution)/shard_map/front/pallas_call | solution.py:460
  48.2 0.0 copy-start.6
  48.3 0.7 %copy-done.6 = f32[256]{0:T(256)S(1)} copy-done((f32[256]{0:T(256)S(1)}, f32[256]{0:T(256)}, u32[]{:S(2)}) %copy-start.6) | copy-done | bytes 1048
  48.9 0.0 copy-start.7
  48.9 0.7 %copy-done.7 = f32[256]{0:T(256)S(1)} copy-done((f32[256]{0:T(256)S(1)}, f32[256]{0:T(256)}, u32[]{:S(2)}) %copy-start.7) | copy-done | bytes 1048
  49.6 0.0 copy-start.10
  49.6 0.7 %copy-done.10 = f32[128]{0:T(128)S(1)} copy-done((f32[128]{0:T(128)S(1)}, f32[128]{0:T(128)}, u32[]{:S(2)}) %copy-start.10) | copy-done | bytes 536
  50.3 3.4 %back.1 = bf16[2,8,40,128]{3,2,1,0:T(8,128)(2,1)} custom-call(f32[27,32,256]{2,1,0:T(8,128)S(1)} %get-tuple-element.8.mid, f32[8,256]{1,0:T(8,128)S(1)} %get-tuple-element.9.moments, bf16[5,640,768]{2,1,0:T(8,128)(2,1)S(1)} %get-tuple-element.10.wc, f32[1,256]{1,0:T(1,128)S(1)} %bitcast.14, f32[1,256]{1,0:T(1,128)S(1)} %bitcast.15, f32[1,128]{1,0:T(1,128)S(1)} %bitcast.18, ...), custom_call_target="tpu_custom_call" | custom-call | tf_op jit(solution)/shard_map/back/pallas_call | solution.py:496
Async XLA Ops:
  0.0 2.0 %copy-start = (bf16[27,256,256]{2,1,0:T(8,128)(2,1)S(1)}, bf16[27,256,256]{2,1,0:T(8,128)(2,1)}, u32[]{:S(2)}) copy-start(bf16[27,256,256]{2,1,0:T(8,128)(2,1)} %hw_hbm.1) | copy-start | bytes 10616836
  2.0 0.9 %copy-start.1 = (bf16[27,256,16]{1,2,0:T(8,128)(2,1)S(1)}, bf16[27,256,16]{1,2,0:T(8,128)(2,1)}, u32[]{:S(2)}) copy-start(bf16[27,256,16]{1,2,0:T(8,128)(2,1)} %param.18) | copy-start | bytes 663556
  2.9 0.7 %copy-start.2 = (bf16[16,256]{1,0:T(8,128)(2,1)S(1)}, bf16[16,256]{1,0:T(8,128)(2,1)}, u32[]{:S(2)}) copy-start(bf16[16,256]{1,0:T(8,128)(2,1)} %wp_hbm.1) | copy-start | bytes 24580
  3.6 0.7 %copy-start.3 = (bf16[2,1,1,5,16]{4,0,3,2,1:T(2,128)(2,1)S(1)}, bf16[2,1,1,5,16]{4,0,3,2,1:T(2,128)(2,1)}, u32[]{:S(2)}) copy-start(bf16[2,1,1,5,16]{4,0,3,2,1:T(2,128)(2,1)} %param.11) | copy-start | bytes 964
  4.3 0.7 %copy-start.4 = (s32[65]{0:T(128)S(1)}, s32[65]{0:T(128)}, u32[]{:S(2)}) copy-start(s32[65]{0:T(128)} %anchors.1) | copy-start | bytes 784
  5.0 0.7 %copy-start.5 = (s32[65]{0:T(128)S(1)}, s32[65]{0:T(128)}, u32[]{:S(2)}) copy-start(s32[65]{0:T(128)} %reach.1) | copy-start | bytes 784
  5.6 0.7 %copy-start.8 = (f32[256]{0:T(256)S(1)}, f32[256]{0:T(256)}, u32[]{:S(2)}) copy-start(f32[256]{0:T(256)} %param.13) | copy-start | bytes 3076
  6.3 0.7 %copy-start.9 = (f32[256]{0:T(256)S(1)}, f32[256]{0:T(256)}, u32[]{:S(2)}) copy-start(f32[256]{0:T(256)} %param.14) | copy-start | bytes 3076
  48.2 0.7 %copy-start.6 = (f32[256]{0:T(256)S(1)}, f32[256]{0:T(256)}, u32[]{:S(2)}) copy-start(f32[256]{0:T(256)} %param.16) | copy-start | bytes 3076
  48.9 0.7 %copy-start.7 = (f32[256]{0:T(256)S(1)}, f32[256]{0:T(256)}, u32[]{:S(2)}) copy-start(f32[256]{0:T(256)} %param.17) | copy-start | bytes 3076
  49.6 0.7 %copy-start.10 = (f32[128]{0:T(128)S(1)}, f32[128]{0:T(128)}, u32[]{:S(2)}) copy-start(f32[128]{0:T(128)} %param.19) | copy-start | bytes 1540

commit v2 on v1

--- a/solution.py
+++ b/solution.py
@@ -88,10 +88,32 @@
     return jnp.clip(other, 0, TILES - 1), (other >= 0) & (other < TILES)
 
 
+def blend_weight(columns, low, high, low_reach, high_reach):
+    left_edge, right_edge = 8 * low, 8 * high
+    left_reach, right_reach = 8 * low_reach, 8 * high_reach
+    place = columns.astype(F32)
+    rising = jnp.clip(
+        (place - (left_edge - left_reach).astype(F32) + 0.5)
+        / jnp.maximum(2 * left_reach, 1).astype(F32),
+        0.0,
+        1.0,
+    )
+    rising = jnp.where(left_reach > 0, rising, jnp.where(columns >= left_edge, 1.0, 0.0))
+    falling = jnp.clip(
+        ((right_edge + right_reach).astype(F32) - place - 0.5)
+        / jnp.maximum(2 * right_reach, 1).astype(F32),
+        0.0,
+        1.0,
+    )
+    falling = jnp.where(right_reach > 0, falling, jnp.where(columns < right_edge, 1.0, 0.0))
+    return jnp.minimum(rising, falling)
+
+
 def front_kernel(
     lat_hbm, wp_hbm, gain_hbm, shift_hbm, hw_hbm, fw_hbm, anchors_hbm, reach_hbm,
-    mid_ref, moments_ref, wc_ref,
-    lbuf, wp, gain, shift, hw, wt, anchors, reach, fl, a1, b1, a2, b2,
+    gain2_hbm, shift2_hbm, bias_hbm,
+    mid_ref, params_ref, inside_ref, blend_ref, wc_ref,
+    lbuf, wp, gain, shift, hw, wt, anchors, reach, gain2, shift2, bias, fl, a1, b1, a2, b2,
     local_sem, sa1, ra1, sb1, rb1, sa2, ra2, sb2, rb2, sl, rl, sw, rw, ss, rs,
 ):
     j = lax.axis_index("tile")
@@ -110,6 +132,9 @@
                 (reach_hbm, reach),
                 (gain_hbm, gain),
                 (shift_hbm, shift),
+                (gain2_hbm, gain2),
+                (shift2_hbm, shift2),
+                (bias_hbm, bias),
                 (hw_hbm.at[pl.ds(0, 9)], hw.at[pl.ds(0, 9)]),
                 (hw_hbm.at[pl.ds(9, 9)], hw.at[pl.ds(9, 9)]),
                 (hw_hbm.at[pl.ds(18, 9)], hw.at[pl.ds(18, 9)]),
@@ -217,6 +242,35 @@
     for load in loads[3:]:
         load.wait()
 
+    params_ref[4:5] = gain2[...]
+    params_ref[5:6] = shift2[...]
+    params_ref[6:7, 0:128] = bias[...]
+    col = 5 * j - 1 + (iota((32, 256), 0) & 7)
+    local_col = iota((32, 256), 0) & 7
+    masks, cores = [], []
+    for k in (-1, 0, 1):
+        t, there = around(j, k)
+        low, high = anchors[t], anchors[t + 1]
+        inside = (col >= low - reach[t]) & (col < high + reach[t + 1])
+        masks.append(jnp.where(inside, 1.0, 0.0))
+        inside_ref[k + 1] = masks[-1][0:16]
+        there = jnp.where(there, 1, 0)
+        core = (col >= low) & (col < high) & (local_col >= 1) & (local_col <= LCW)
+        cores.append(jnp.where(core, there.astype(F32), 0.0))
+
+    for c in range(8):
+        columns = 40 * j - 8 + 8 * iota((8, 128), 0) + c
+        parts = []
+        for k in range(3):
+            t, there = around(j, k - 1)
+            weight = blend_weight(columns, anchors[t], anchors[t + 1], reach[t], reach[t + 1])
+            parts.append(weight * jnp.where(there, 1, 0).astype(F32))
+        total = parts[0] + parts[1] + parts[2]
+        keep = (iota((8, 128), 0) >= 1) & (iota((8, 128), 0) <= LCW)
+        total = jnp.where(keep, total, 1.0)
+        for k in range(3):
+            blend_ref[3 * c + k] = parts[k] / total
+
     for copy in first_plane:
         copy.wait_recv()
     totals = [jnp.sum(b1[8 * s : 8 * s + 8], axis=0) for s in range(3)]
@@ -232,18 +286,6 @@
     frames[0] = jnp.where(tm == 1, frames[2], frames[0])
     frames[1] = jnp.where(tm == 1, frames[2], frames[1])
     seqs = [jnp.concatenate(frames[a : a + 4], axis=0).astype(BF) for a in range(3)]
-
-    col = 5 * j - 1 + (iota((32, 256), 0) & 7)
-    local_col = iota((32, 256), 0) & 7
-    masks, cores = [], []
-    for k in (-1, 0, 1):
-        t, there = around(j, k)
-        low, high = anchors[t], anchors[t + 1]
-        inside = (col >= low - reach[t]) & (col < high + reach[t + 1])
-        masks.append(jnp.where(inside, 1.0, 0.0))
-        there = jnp.where(there, 1, 0)
-        core = (col >= low) & (col < high) & (local_col >= 1) & (local_col <= LCW)
-        cores.append(jnp.where(core, there.astype(F32), 0.0))
 
     taps = [
         [
@@ -325,53 +367,30 @@
         copy.wait_recv()
     totals = [jnp.sum(b2[8 * s : 8 * s + 8], axis=0) for s in range(2)]
     stats = decode(totals, float(2 * 16 * LCW * TILES * 8))
-    moments_ref[0:1] = stats[1][0]
-    moments_ref[1:2] = stats[1][1]
-    moments_ref[2:3] = stats[0][0]
-    moments_ref[3:4] = stats[0][1]
+    params_ref[0:1] = stats[1][0]
+    params_ref[1:2] = stats[1][1]
+    params_ref[2:3] = stats[0][0]
+    params_ref[3:4] = stats[0][1]
     for copy in (
         first_column + lat_copies + first_plane + chip_copies + second_column + sibling_copies + second_plane
     ):
         copy.wait_send()
 
 
-def blend_weight(columns, low, high, low_reach, high_reach):
-    left_edge, right_edge = 8 * low, 8 * high
-    left_reach, right_reach = 8 * low_reach, 8 * high_reach
-    place = columns.astype(F32)
-    rising = jnp.clip(
-        (place - (left_edge - left_reach).astype(F32) + 0.5)
-        / jnp.maximum(2 * left_reach, 1).astype(F32),
-        0.0,
-        1.0,
-    )
-    rising = jnp.where(left_reach > 0, rising, jnp.where(columns >= left_edge, 1.0, 0.0))
-    falling = jnp.clip(
-        ((right_edge + right_reach).astype(F32) - place - 0.5)
-        / jnp.maximum(2 * right_reach, 1).astype(F32),
-        0.0,
-        1.0,
-    )
-    falling = jnp.where(right_reach > 0, falling, jnp.where(columns < right_edge, 1.0, 0.0))
-    return jnp.minimum(rising, falling)
-
-
 def back_kernel(
-    mid, moments, wc, gain, shift, bias, anchors, reach, out_ref, xs, acc, rows
+    mid, params, inside, blend, wc, out_ref, xs, acc, rows
 ):
-    j = lax.axis_index("tile")
     tm = lax.axis_index("tm")
-    col = 5 * j - 1 + (iota((16, 256), 0) & 7)
+    gain, shift, bias = params[4:5], params[5:6], params[6:7, 0:128]
     for k in range(3):
-        t, _ = around(j, k - 1)
-        inside = (col >= anchors[t] - reach[t]) & (col < anchors[t + 1] + reach[t + 1])
+        keep = inside[k]
         for r in range(3):
             for p in range(3):
                 values = mid[k * 9 + r * 3 + p]
-                before = normalize(values[0:16], moments[0:1], moments[1:2], gain[...], shift[...])
-                now = normalize(values[16:32], moments[2:3], moments[3:4], gain[...], shift[...])
-                now = jnp.where(inside, now, 0.0)
-                before = jnp.where(inside, before, 0.0)
+                before = normalize(values[0:16], params[0:1], params[1:2], gain, shift)
+                now = normalize(values[16:32], params[2:3], params[3:4], gain, shift)
+                now = keep * now
+                before = keep * before
                 first = jnp.concatenate([now[0:8], now[0:8]], axis=0)
                 before = jnp.where(tm == 0, first, before)
                 at = (r * 3 + p) * 48 + k * 16
@@ -409,19 +428,6 @@
                             seen.add(slot)
                             acc[slot] = part
 
-    weights = []
-    for c in range(8):
-        columns = 40 * j - 8 + 8 * iota((8, 128), 0) + c
-        parts = []
-        for k in range(3):
-            t, there = around(j, k - 1)
-            weight = blend_weight(columns, anchors[t], anchors[t + 1], reach[t], reach[t + 1])
-            parts.append(weight * jnp.where(there, 1, 0).astype(F32))
-        total = parts[0] + parts[1] + parts[2]
-        keep = (iota((8, 128), 0) >= 1) & (iota((8, 128), 0) <= LCW)
-        total = jnp.where(keep, total, 1.0)
-        weights.append([part / total for part in parts])
-
     for t in range(2):
         for big_row in (0, 1, 2, 3, 5, 6, 7):
             for c in range(8):
@@ -429,7 +435,7 @@
                 value = None
                 for k in range(3):
                     at = k * 16 + t * 8
-                    piece = (acc[slot, at : at + 8] + bias[...]).astype(BF).astype(F32) * weights[c][k]
+                    piece = (acc[slot, at : at + 8] + bias).astype(BF).astype(F32) * blend[3 * c + k]
                     value = piece if value is None else value + piece
                 rows[pl.ds(c, 8, stride=8), :] = value
             final = rows[8:48].astype(BF)
@@ -455,18 +461,19 @@
     shard = full_weight.transpose(0, 2, 1)
     any_space = pl.BlockSpec(memory_space=pl.ANY)
     vmem = pl.BlockSpec(memory_space=pltpu.VMEM)
-    smem = pl.BlockSpec(memory_space=pltpu.SMEM)
     dma = pltpu.SemaphoreType.DMA
-    mid, moments, wc = pl.pallas_call(
+    held = pl.pallas_call(
         front_kernel,
         name="front",
         out_shape=(
             jax.ShapeDtypeStruct((27, 32, 256), F32),
             jax.ShapeDtypeStruct((8, 256), F32),
+            jax.ShapeDtypeStruct((3, 16, 256), F32),
+            jax.ShapeDtypeStruct((24, 8, 128), F32),
             jax.ShapeDtypeStruct((5, 640, 768), BF),
         ),
-        in_specs=[any_space] * 8,
-        out_specs=(vmem, vmem, vmem),
+        in_specs=[any_space] * 11,
+        out_specs=(vmem,) * 5,
         scratch_shapes=[
             pltpu.VMEM((3, LCW + 2, 2, 16), BF),
             pltpu.VMEM((16, 256), BF),
@@ -476,12 +483,15 @@
             pltpu.VMEM((NT, 27, 16, 256), BF),
             pltpu.SMEM((TILES + 1,), jnp.int32),
             pltpu.SMEM((TILES + 1,), jnp.int32),
+            pltpu.VMEM((1, 256), F32),
+            pltpu.VMEM((1, 256), F32),
+            pltpu.VMEM((1, 128), F32),
             pltpu.VMEM((48, 16), F32),
             pltpu.VMEM((8, 1, 128), F32),
             pltpu.VMEM((24, 1, 128), F32),
             pltpu.VMEM((8, 1, 128), F32),
             pltpu.VMEM((16, 1, 128), F32),
-            dma((10,)),
+            dma((13,)),
             dma((8,)), dma((8,)), dma((24,)), dma((24,)),
             dma((8,)), dma((8,)), dma((16,)), dma((16,)),
             dma((9,)), dma((9,)), dma((4,)), dma((4,)), dma((4,)), dma((4,)),
@@ -490,14 +500,20 @@
             collective_id=0, has_side_effects=True, vmem_limit_bytes=20 * 2**20
         ),
     )(
-        lat, proj_weight, first_gain.reshape(1, 256), first_shift.reshape(1, 256),
-        half_weight, shard, anchors, reach,
+        *(
+            pltpu.with_memory_space_constraint(v, pltpu.HBM)
+            for v in (
+                lat, proj_weight, first_gain.reshape(1, 256), first_shift.reshape(1, 256),
+                half_weight, shard, anchors, reach,
+                second_gain.reshape(1, 256), second_shift.reshape(1, 256), full_bias.reshape(1, 128),
+            )
+        )
     )
     out = pl.pallas_call(
         back_kernel,
         name="back",
         out_shape=jax.ShapeDtypeStruct((2, 8, 8 * LCW, 128), BF),
-        in_specs=[vmem] * 6 + [smem] * 2,
+        in_specs=[vmem] * 5,
         out_specs=vmem,
         scratch_shapes=[
             pltpu.VMEM((432, 768), BF),
@@ -505,10 +521,7 @@
             pltpu.VMEM((64, 128), F32),
         ],
         compiler_params=pltpu.CompilerParams(vmem_limit_bytes=20 * 2**20),
-    )(
-        mid, moments, wc, second_gain.reshape(1, 256), second_shift.reshape(1, 256),
-        full_bias.reshape(1, 128), anchors, reach,
-    )
+    )(*held)
     return out[:, None]
 
 

time: 54 us -> 43.4 us (0.80)
  local copies, waits for them, and re-layouts: 8.99 us -> 0 us
  Pallas kernels: 44.7 us -> 43.2 us
    unnamed x22 -> x0, local copies, waits for them, and re-layouts: 8.99 us -> none
    pallas_call x1, Pallas kernels: 41.2 us -> 40.3 us  [on_device(): pl.pallas_call(front_kernel, name='front', out_shape=(jax.ShapeDtypeStruc...]
where the time goes in v2:
time: 43.4 us; the launch traced here: 43.2 us
  Pallas kernels  43.2 us (100%)
    pallas_call x1, Pallas kernels, on_device(): pl.pallas_call(front_kernel, name='front', out_shape=(jax.ShapeDtypeStruc...  40.3 us
    pallas_call x1, Pallas kernels, on_device(): pl.pallas_call(back_kernel, name='back', out_shape=jax.ShapeDtypeStruct((...  2.95 us

profile of v2, /device:TPU:1, one launch (start us, length us, event | category | flops | bytes accessed | tf_op | source)
XLA Modules:
  0.0 43.2 jit_solution(3888818871801920227)
XLA Ops:
  0.0 40.3 %front.1 = (f32[27,32,256]{2,1,0:T(8,128)S(1)}, f32[8,256]{1,0:T(8,128)S(1)}, f32[3,16,256]{2,1,0:T(8,128)S(1)}, f32[24,8,128]{2,1,0:T(8,128)S(1)}, bf16[5,640,768]{2,1,0:T(8,128)(2,1)S(1)}) custom-call(bf16[5,2,16]{2,1,0:T(2,128)(2,1)} %bitcast.13, bf16[16,256]{1,0:T(8,128)(2,1)} %wp_hbm.1, f32[1,256]{1,0:T(1,128)} %bitcast.14, f32[1,256]{1,0:T(1,128)} %bitcast.15, ...), custom_call_target="tpu_custom_call" | custom-call | tf_op jit(solution)/shard_map/front/pallas_call | solution.py:465
  40.3 2.9 %back.1 = bf16[2,8,40,128]{3,2,1,0:T(8,128)(2,1)} custom-call(f32[27,32,256]{2,1,0:T(8,128)S(1)} %get-tuple-element.10.mid, f32[8,256]{1,0:T(8,128)S(1)} %get-tuple-element.11.params, f32[3,16,256]{2,1,0:T(8,128)S(1)} %get-tuple-element.12.inside, f32[24,8,128]{2,1,0:T(8,128)S(1)} %get-tuple-element.13.blend, bf16[5,640,768]{2,1,0:T(8,128)(2,1)S(1)} %get-tuple-element.14.wc), custom_call_target="tpu_custom_call" | custom-call | tf_op jit(solution)/shard_map/back/pallas_call | solution.py:512

commit v3 on v2

--- a/solution.py
+++ b/solution.py
@@ -12,23 +12,6 @@
 BF = jnp.bfloat16
 F32 = jnp.float32
 MESH = pl.DeviceIdType.MESH
-
-COMBOS = ("01", "12", "0", "2", "012")
-ROW_USES = {
-    "01": ((0, 1), (1, 5), (2, 7)),
-    "12": ((0, 0), (1, 2), (2, 6)),
-    "0": ((0, 2), (1, 6)),
-    "2": ((1, 1), (2, 5)),
-    "012": ((1, 3),),
-}
-COL_USES = {
-    "01": ((0, 1, 0), (1, 5, 0), (2, 7, 0)),
-    "12": ((0, 0, 0), (1, 2, 0), (2, 6, 0)),
-    "0": ((0, 2, 0), (1, 6, 0), (2, 0, 1)),
-    "2": ((0, 7, -1), (1, 1, 0), (2, 5, 0)),
-    "012": ((1, 3, 0),),
-}
-SLOT = {0: 0, 1: 1, 2: 2, 3: 3, 4: 3, 5: 4, 6: 5, 7: 6}
 
 
 def dot(a, b):
@@ -125,7 +108,7 @@
         pltpu.make_async_copy(src, dst, local_sem.at[i])
         for i, (src, dst) in enumerate(
             (
-                (lat_hbm, lbuf.at[0, pl.ds(1, LCW)]),
+                (lat_hbm, lbuf.at[pl.ds(1, LCW)]),
                 (wp_hbm, wp),
                 (fw_hbm, wt.at[tm]),
                 (anchors_hbm, anchors),
@@ -172,72 +155,61 @@
     loads[0].wait()
     loads[1].wait()
     for c in range(LCW):
-        fl[pl.ds(32 + 1 + c, 2, stride=8), :] = lbuf[0, 1 + c].astype(F32)
+        fl[pl.ds(32 + 1 + c, 2, stride=8), :] = lbuf[1 + c].astype(F32)
     own = dot(fl[32:48].astype(BF), wp[...])
     a1[0] = encode(jnp.sum(own, axis=0, keepdims=True), jnp.sum(own * own, axis=0, keepdims=True))
 
     pl.semaphore_wait(barrier, len(greeted))
 
     def send(src, dst, send_sem, recv_sem, peer):
-        copy = pltpu.make_async_remote_copy(
+        pltpu.make_async_remote_copy(
             src_ref=src, dst_ref=dst, send_sem=send_sem, recv_sem=recv_sem,
             device_id=peer, device_id_type=MESH,
-        )
-        copy.start()
-        return copy
+        ).start()
+
+    def await_all(part, sem):
+        pltpu.make_async_copy(part, part, sem).wait()
 
     def send_column(buf, s_sem, r_sem):
-        return [send(buf.at[0], buf.at[d], s_sem.at[d], r_sem.at[d], column[d]) for d in range(1, NY)]
+        for d in range(1, NY):
+            send(buf.at[0], buf.at[d], s_sem, r_sem, column[d])
 
     def send_plane(buf, s_sem, r_sem, shifts):
-        copies = []
         for s, dz, dx in plane:
             if s < shifts:
-                i = s * 8 + dz * NX + dx
-                copies.append(
-                    send(buf.at[0], buf.at[i], s_sem.at[i], r_sem.at[i], plane_at(1, s, dz, dx))
-                )
-        return copies
-
-    sent = []
-    first_column = send_column(a1, sa1, ra1)
-    lat_copies = []
+                send(buf.at[0], buf.at[s * 8 + dz * NX + dx], s_sem, r_sem, plane_at(1, s, dz, dx))
+
+    send_column(a1, sa1, ra1)
     for s in range(3):
+        first = s * (LCW + 2)
         for i, (src, dst, tile) in enumerate(
             (
-                (lbuf.at[0, LCW], lbuf.at[s, 0], (j + 1) % TILES),
-                (lbuf.at[0, 1], lbuf.at[s, LCW + 1], (j + TILES - 1) % TILES),
-                (lbuf.at[0, pl.ds(1, LCW)], lbuf.at[s, pl.ds(1, LCW)], j),
+                (lbuf.at[LCW], lbuf.at[first], (j + 1) % TILES),
+                (lbuf.at[1], lbuf.at[first + LCW + 1], (j + TILES - 1) % TILES),
+                (lbuf.at[pl.ds(1, LCW)], lbuf.at[pl.ds(first + 1, LCW)], j),
             )
         ):
             if i == 2 and s == 0:
                 continue
-            n = 3 * s + i
-            lat_copies.append(send(src, dst, sl.at[n], rl.at[n], (tile, (tm + s) % NT)))
+            send(src, dst, sl, rl, (tile, (tm + s) % NT))
     loads[2].wait()
-    sibling_copies = [send(wt.at[tm], wt.at[tm], ss.at[0], rs.at[0], sibling)]
-
-    for copy in first_column:
-        copy.wait_recv()
+    send(wt.at[tm], wt.at[tm], ss, rs, sibling)
+
+    await_all(a1.at[pl.ds(1, 7)], ra1)
     b1[0] = jnp.sum(a1[...], axis=0)
-    first_plane = send_plane(b1, sb1, rb1, 3)
+    send_plane(b1, sb1, rb1, 3)
 
     half = 14
-    chip_copies = [
-        send(wt.at[tm], wt.at[tm], sw.at[0], rw.at[0], chips[0]),
-        send(wt.at[tm], wt.at[tm], sw.at[1], rw.at[1], chips[1]),
-        send(wt.at[tm, pl.ds(0, half)], wt.at[tm, pl.ds(0, half)], sw.at[2], rw.at[2], chips[2]),
-        send(
-            wt.at[tm, pl.ds(half, 27 - half)], wt.at[tm, pl.ds(half, 27 - half)],
-            sw.at[3], rw.at[3], chips[3],
-        ),
-    ]
-
-    for copy in lat_copies:
-        copy.wait_recv()
+    send(wt.at[tm], wt.at[tm], sw, rw, chips[0])
+    send(wt.at[tm], wt.at[tm], sw, rw, chips[1])
+    for first, many, chip in ((0, half, chips[2]), (half, 27 - half, chips[3])):
+        part = wt.at[tm, pl.ds(first, many)]
+        send(part, part, sw, rw, chip)
+
+    await_all(lbuf.at[pl.ds(0, 16)], rl)
     for s in range(3):
         for c in range(LCW + 2):
-            fl[pl.ds(16 * (2 - s) + c, 2, stride=8), :] = lbuf[s, c].astype(F32)
+            fl[pl.ds(16 * (2 - s) + c, 2, stride=8), :] = lbuf[s * (LCW + 2) + c].astype(F32)
     projected = dot(fl[...].astype(BF), wp[...])
     for load in loads[3:]:
         load.wait()
@@ -271,8 +243,7 @@
         for k in range(3):
             blend_ref[3 * c + k] = parts[k] / total
 
-    for copy in first_plane:
-        copy.wait_recv()
+    await_all(b1.at[pl.ds(1, 23)], rb1)
     totals = [jnp.sum(b1[8 * s : 8 * s + 8], axis=0) for s in range(3)]
     stats = decode(totals, float(2 * LCW * TILES * 8))
     frames = []
@@ -325,60 +296,49 @@
                 sums = sums + times * (part[0:8] + part[8:16])
                 squares = squares + times * (square[0:8] + square[8:16])
     a2[0] = encode(jnp.sum(sums, axis=0, keepdims=True), jnp.sum(squares, axis=0, keepdims=True))
-    second_column = send_column(a2, sa2, ra2)
-
-    for copy in chip_copies:
-        copy.wait_recv()
-    for i, shard in enumerate(((tm + 2) % NT, (tm + 4) % NT, (tm + 6) % NT)):
-        sibling_copies.append(
-            send(wt.at[shard], wt.at[shard], ss.at[1 + i], rs.at[1 + i], sibling)
-        )
-
-    for copy in second_column:
-        copy.wait_recv()
+    send_column(a2, sa2, ra2)
+
+    await_all(wt.at[pl.ds(0, 3)], rw)
+    for shard in ((tm + 2) % NT, (tm + 4) % NT, (tm + 6) % NT):
+        send(wt.at[shard], wt.at[shard], ss, rs, sibling)
+
+    await_all(a2.at[pl.ds(1, 7)], ra2)
     b2[0] = jnp.sum(a2[...], axis=0)
-    second_plane = send_plane(b2, sb2, rb2, 2)
-
-    for copy in sibling_copies:
-        copy.wait_recv()
-
-    def combine(i, carry):
-        a, n = i // NT, i % NT
-        w = [[wt[n, 9 * a + 3 * b + d].astype(F32) for d in range(3)] for b in range(3)]
-
-        def combos(u):
-            first = u[0] + u[1]
-            return {"0": u[0], "2": u[2], "01": first, "12": u[1] + u[2], "012": first + u[2]}
-
-        by_col = [combos([w[b][d] for b in range(3)]) for d in range(3)]
-        for rc, row_class in enumerate(COMBOS):
-            both = combos([by_col[d][row_class] for d in range(3)])
-            for cc, col_class in enumerate(COMBOS):
+    send_plane(b2, sb2, rb2, 2)
+
+    await_all(wt.at[pl.ds(0, 4)], rs)
+
+    def arrange(n, carry):
+        for tap in range(9):
+            for a in range(3):
                 wc_ref[
-                    rc,
-                    pl.ds(pl.multiple_of(cc * 128 + n * 16, 16), 16),
-                    pl.ds(pl.multiple_of(a * 256, 256), 256),
-                ] = both[col_class].astype(BF)
+                    pl.ds(pl.multiple_of(tap * 128 + n * 16, 16), 16), a * 256 : a * 256 + 256
+                ] = wt[n, 9 * a + tap]
         return carry
 
-    lax.fori_loop(0, 3 * NT, combine, 0)
-
-    for copy in second_plane:
-        copy.wait_recv()
+    lax.fori_loop(0, NT, arrange, 0)
+
+    await_all(b2.at[pl.ds(1, 15)], rb2)
     totals = [jnp.sum(b2[8 * s : 8 * s + 8], axis=0) for s in range(2)]
     stats = decode(totals, float(2 * 16 * LCW * TILES * 8))
     params_ref[0:1] = stats[1][0]
     params_ref[1:2] = stats[1][1]
     params_ref[2:3] = stats[0][0]
     params_ref[3:4] = stats[0][1]
-    for copy in (
-        first_column + lat_copies + first_plane + chip_copies + second_column + sibling_copies + second_plane
+    for part, sem in (
+        (a1.at[pl.ds(1, 7)], sa1),
+        (b1.at[pl.ds(1, 23)], sb1),
+        (lbuf.at[pl.ds(0, 16)], sl),
+        (wt.at[pl.ds(0, 3)], sw),
+        (wt.at[pl.ds(0, 4)], ss),
+        (a2.at[pl.ds(1, 7)], sa2),
+        (b2.at[pl.ds(1, 15)], sb2),
     ):
-        copy.wait_send()
+        await_all(part, sem)
 
 
 def back_kernel(
-    mid, params, inside, blend, wc, out_ref, xs, acc, rows
+    mid, params, inside, blend, wc, out_ref, xs, prod, rows
 ):
     tm = lax.axis_index("tm")
     gain, shift, bias = params[4:5], params[5:6], params[6:7, 0:128]
@@ -398,50 +358,64 @@
                 xs[at : at + 16, 256:512] = jnp.concatenate([before[8:16], now[0:8]], axis=0).astype(BF)
                 xs[at : at + 16, 512:768] = now.astype(BF)
 
-    seen = set()
-    for rc, row_class in enumerate(COMBOS):
-        uses = ROW_USES[row_class]
-        r0, r1 = uses[0][0], uses[-1][0] + 1
-        for pair in ((0, 1), (2, 3), (4,)):
-            if pair == (4,):
-                lhs = [xs[r * 144 + 48 : r * 144 + 96] for r in range(r0, r1)]
-                lhs = lhs[0] if len(lhs) == 1 else jnp.concatenate(lhs, axis=0)
-                inputs = (1,)
-            else:
-                lhs = xs[r0 * 144 : r1 * 144]
-                inputs = (0, 1, 2)
-            rhs = wc[rc, pair[0] * 128 : (pair[-1] + 1) * 128]
-            result = lax.dot_general(
-                lhs, rhs, (((1,), (1,)), ((), ())), preferred_element_type=F32
-            )
-            for r, big_row in uses:
-                for half, cc in enumerate(pair):
-                    for p, big_col, by in COL_USES[COMBOS[cc]]:
-                        at = ((r - r0) * len(inputs) + inputs.index(p)) * 48
-                        part = result[at : at + 48, half * 128 : half * 128 + 128]
-                        if by:
-                            part = pltpu.roll(part.reshape(6, 8, 128), by % 8, 1).reshape(48, 128)
-                        slot = SLOT[big_row] * 7 + SLOT[big_col]
-                        if slot in seen:
-                            acc[slot] += part
+    for n in range(0, 9, 2):
+        many = min(2, 9 - n)
+        result = lax.dot_general(
+            xs[...], wc[n * 128 : (n + many) * 128], (((1,), (1,)), ((), ())), preferred_element_type=F32
+        )
+        for i in range(many):
+            prod[n + i] = result[:, i * 128 : i * 128 + 128]
+
+    def products(b, r, at):
+        return [
+            [prod[3 * b + d, (r * 3 + p) * 48 + at : (r * 3 + p) * 48 + at + 8] for p in range(3)]
+            for d in range(3)
+        ]
+
+    for t in range(2):
+        for k in range(3):
+            at = k * 16 + t * 8
+            across = {}
+            for b in range(3):
+                for r in range(3):
+                    (a0, a1, a3), (b0, b1, b3), (c0, c1, c3) = products(b, r, at)
+                    ab1, bc1 = a1 + b1, b1 + c1
+                    across[b, r] = (
+                        pltpu.roll(a3, 1, 0) + (b0 + c0),
+                        (a0 + b0) + c1,
+                        a0 + bc1,
+                        ab1 + c1,
+                        ab1 + c3,
+                        a1 + (b3 + c3),
+                        (a3 + b3) + pltpu.roll(c0, 7, 0),
+                    )
+            for c in range(7):
+                (x0, x1, x3), (y0, y1, y3), (z0, z1, z3) = [
+                    [across[b, r][c] for r in range(3)] for b in range(3)
+                ]
+                xy1, yz1 = x1 + y1, y1 + z1
+                down = (
+                    y0 + z0,
+                    (x0 + y0) + z1,
+                    x0 + yz1,
+                    xy1 + z1,
+                    xy1 + z3,
+                    x1 + (y3 + z3),
+                    x3 + y3,
+                )
+                for r in range(7):
+                    value = (down[r] + bias).astype(BF).astype(F32)
+                    for column in (3, 4) if c == 3 else (c if c < 3 else c + 1,):
+                        place = pl.ds(column, 8, stride=8)
+                        piece = value * blend[3 * column + k]
+                        if k == 0:
+                            rows[r, place, :] = piece
                         else:
-                            seen.add(slot)
-                            acc[slot] = part
-
-    for t in range(2):
-        for big_row in (0, 1, 2, 3, 5, 6, 7):
-            for c in range(8):
-                slot = SLOT[big_row] * 7 + SLOT[c]
-                value = None
-                for k in range(3):
-                    at = k * 16 + t * 8
-                    piece = (acc[slot, at : at + 8] + bias).astype(BF).astype(F32) * blend[3 * c + k]
-                    value = piece if value is None else value + piece
-                rows[pl.ds(c, 8, stride=8), :] = value
-            final = rows[8:48].astype(BF)
-            out_ref[t, big_row] = final
-            if big_row == 3:
-                out_ref[t, 4] = final
+                            rows[r, place, :] += piece
+        for r in range(7):
+            final = rows[r, 8:48].astype(BF)
+            for big_row in (3, 4) if r == 3 else (r if r < 3 else r + 1,):
+                out_ref[t, big_row] = final
 
 
 def on_device(
@@ -470,12 +444,12 @@
             jax.ShapeDtypeStruct((8, 256), F32),
             jax.ShapeDtypeStruct((3, 16, 256), F32),
             jax.ShapeDtypeStruct((24, 8, 128), F32),
-            jax.ShapeDtypeStruct((5, 640, 768), BF),
+            jax.ShapeDtypeStruct((9 * 128, 768), BF),
         ),
         in_specs=[any_space] * 11,
         out_specs=(vmem,) * 5,
         scratch_shapes=[
-            pltpu.VMEM((3, LCW + 2, 2, 16), BF),
+            pltpu.VMEM((3 * (LCW + 2), 2, 16), BF),
             pltpu.VMEM((16, 256), BF),
             pltpu.VMEM((1, 256), F32),
             pltpu.VMEM((1, 256), F32),
@@ -492,9 +466,7 @@
             pltpu.VMEM((8, 1, 128), F32),
             pltpu.VMEM((16, 1, 128), F32),
             dma((13,)),
-            dma((8,)), dma((8,)), dma((24,)), dma((24,)),
-            dma((8,)), dma((8,)), dma((16,)), dma((16,)),
-            dma((9,)), dma((9,)), dma((4,)), dma((4,)), dma((4,)), dma((4,)),
+            *[dma] * 14,
         ],
         compiler_params=pltpu.CompilerParams(
             collective_id=0, has_side_effects=True, vmem_limit_bytes=20 * 2**20
@@ -517,8 +489,8 @@
         out_specs=vmem,
         scratch_shapes=[
             pltpu.VMEM((432, 768), BF),
-            pltpu.VMEM((49, 48, 128), F32),
-            pltpu.VMEM((64, 128), F32),
+            pltpu.VMEM((9, 432, 128), F32),
+            pltpu.VMEM((7, 64, 128), F32),
         ],
         compiler_params=pltpu.CompilerParams(vmem_limit_bytes=20 * 2**20),
     )(*held)

time: 43.4 us -> 41.4 us (0.954)
  Pallas kernels: 43.2 us -> 41.3 us
    pallas_call x1, Pallas kernels: 40.3 us -> 39 us  [on_device(): pl.pallas_call(front_kernel, name='front', out_shape=(jax.ShapeDtypeStruc...]
    pallas_call x1, Pallas kernels: 2.95 us -> 2.32 us  [on_device(): pl.pallas_call(back_kernel, name='back', out_shape=jax.ShapeDtypeStruct((...]
where the time goes in v3:
time: 41.4 us; the launch traced here: 41.3 us
  Pallas kernels  41.3 us (100%)
    pallas_call x1, Pallas kernels, on_device(): pl.pallas_call(front_kernel, name='front', out_shape=(jax.ShapeDtypeStruc...  39 us
    pallas_call x1, Pallas kernels, on_device(): pl.pallas_call(back_kernel, name='back', out_shape=jax.ShapeDtypeStruct((...  2.32 us

profile of v3, /device:TPU:1, one launch (start us, length us, event | category | flops | bytes accessed | tf_op | source)
XLA Modules:
  0.0 41.3 jit_solution(7677462753626747403)
XLA Ops:
  0.0 39.0 %front.1 = (f32[27,32,256]{2,1,0:T(8,128)S(1)}, f32[8,256]{1,0:T(8,128)S(1)}, f32[3,16,256]{2,1,0:T(8,128)S(1)}, f32[24,8,128]{2,1,0:T(8,128)S(1)}, bf16[1152,768]{1,0:T(8,128)(2,1)S(1)}) custom-call(bf16[5,2,16]{2,1,0:T(2,128)(2,1)} %bitcast.13, bf16[16,256]{1,0:T(8,128)(2,1)} %wp_hbm.1, f32[1,256]{1,0:T(1,128)} %bitcast.14, f32[1,256]{1,0:T(1,128)} %bitcast.15, ...), custom_call_target="tpu_custom_call" | custom-call | tf_op jit(solution)/shard_map/front/pallas_call | solution.py:439
  39.0 2.3 %back.1 = bf16[2,8,40,128]{3,2,1,0:T(8,128)(2,1)} custom-call(f32[27,32,256]{2,1,0:T(8,128)S(1)} %get-tuple-element.10.mid, f32[8,256]{1,0:T(8,128)S(1)} %get-tuple-element.11.params, f32[3,16,256]{2,1,0:T(8,128)S(1)} %get-tuple-element.12.inside, f32[24,8,128]{2,1,0:T(8,128)S(1)} %get-tuple-element.13.blend, bf16[1152,768]{1,0:T(8,128)(2,1)S(1)} %get-tuple-element.14.wc), custom_call_target="tpu_custom_call" | custom-call | tf_op jit(solution)/shard_map/back/pallas_call | solution.py:484

commit v4 on v3

--- a/solution.py
+++ b/solution.py
@@ -96,8 +96,8 @@
     lat_hbm, wp_hbm, gain_hbm, shift_hbm, hw_hbm, fw_hbm, anchors_hbm, reach_hbm,
     gain2_hbm, shift2_hbm, bias_hbm,
     mid_ref, params_ref, inside_ref, blend_ref, wc_ref,
-    lbuf, wp, gain, shift, hw, wt, anchors, reach, gain2, shift2, bias, fl, a1, b1, a2, b2,
-    local_sem, sa1, ra1, sb1, rb1, sa2, ra2, sb2, rb2, sl, rl, sw, rw, ss, rs,
+    lbuf, wp, gain, shift, hw, wt, anchors, reach, gain2, shift2, bias, fl, a1, b1, b2,
+    local_sem, sa1, ra1, sb1, rb1, sb2, rb2, sl, rl, sw, rw, ss, rs,
 ):
     j = lax.axis_index("tile")
     tm = lax.axis_index("tm")
@@ -128,12 +128,18 @@
         load.start()
 
     column = [(tile_at((y + d) % NY, z, x), tm) for d in range(NY)]
-    plane = [(s, dz, dx) for s in range(3) for dz in range(NZH) for dx in range(NX)][1:]
-
-    def plane_at(sign, s, dz, dx):
+    shifts = (0, 1, 2, -1)
+    plane = [(i, dz, dx) for i in range(4) for dz in range(NZH) for dx in range(NX)][1:]
+    plane.sort(key=lambda p: -(4 * p[1] + min(p[2], NX - p[2])))
+    everyone = [
+        (s, dy, dz, dx) for s in range(2) for dy in range(NY) for dz in range(NZH) for dx in range(NX)
+    ][1:]
+    everyone.sort(key=lambda p: -(min(p[1], NY - p[1]) + 4 * p[2] + min(p[3], NX - p[3])))
+
+    def plane_at(sign, i, dz, dx):
         return (
             tile_at(y, (z + dz) % NZH, (x + sign * dx + NX) % NX),
-            (tm + sign * s + NT) % NT,
+            (tm + sign * shifts[i] + NT) % NT,
         )
 
     def chip_at(step):
@@ -144,10 +150,11 @@
     chips = [chip_at(1), chip_at(-1), chip_at(2), chip_at(-2)]
 
     barrier = pltpu.get_barrier_semaphore()
-    greeted = column[1:] + [plane_at(-1, *p) for p in plane] + chips + [sibling]
+    greeted = []
     for s in range(3):
         greeted.append(((j + 1) % TILES, (tm - s + NT) % NT))
         greeted.append(((j + TILES - 1) % TILES, (tm - s + NT) % NT))
+    greeted += [plane_at(-1, *p) for p in plane] + column[1:] + chips + [sibling]
     for peer in greeted:
         pl.semaphore_signal(barrier, inc=1, device_id=peer, device_id_type=MESH)
 
@@ -171,13 +178,8 @@
         pltpu.make_async_copy(part, part, sem).wait()
 
     def send_column(buf, s_sem, r_sem):
-        for d in range(1, NY):
+        for d in (4, 3, 5, 2, 6, 1, 7):
             send(buf.at[0], buf.at[d], s_sem, r_sem, column[d])
-
-    def send_plane(buf, s_sem, r_sem, shifts):
-        for s, dz, dx in plane:
-            if s < shifts:
-                send(buf.at[0], buf.at[s * 8 + dz * NX + dx], s_sem, r_sem, plane_at(1, s, dz, dx))
 
     send_column(a1, sa1, ra1)
     for s in range(3):
@@ -197,7 +199,8 @@
 
     await_all(a1.at[pl.ds(1, 7)], ra1)
     b1[0] = jnp.sum(a1[...], axis=0)
-    send_plane(b1, sb1, rb1, 3)
+    for i, dz, dx in plane:
+        send(b1.at[0], b1.at[8 * i + dz * NX + dx], sb1, rb1, plane_at(1, i, dz, dx))
 
     half = 14
     send(wt.at[tm], wt.at[tm], sw, rw, chips[0])
@@ -217,15 +220,15 @@
     params_ref[4:5] = gain2[...]
     params_ref[5:6] = shift2[...]
     params_ref[6:7, 0:128] = bias[...]
-    col = 5 * j - 1 + (iota((32, 256), 0) & 7)
-    local_col = iota((32, 256), 0) & 7
+    col = 5 * j - 1 + (iota((16, 256), 0) & 7)
+    local_col = iota((16, 256), 0) & 7
     masks, cores = [], []
     for k in (-1, 0, 1):
         t, there = around(j, k)
         low, high = anchors[t], anchors[t + 1]
         inside = (col >= low - reach[t]) & (col < high + reach[t + 1])
         masks.append(jnp.where(inside, 1.0, 0.0))
-        inside_ref[k + 1] = masks[-1][0:16]
+        inside_ref[k + 1] = masks[-1]
         there = jnp.where(there, 1, 0)
         core = (col >= low) & (col < high) & (local_col >= 1) & (local_col <= LCW)
         cores.append(jnp.where(core, there.astype(F32), 0.0))
@@ -243,68 +246,74 @@
         for k in range(3):
             blend_ref[3 * c + k] = parts[k] / total
 
-    await_all(b1.at[pl.ds(1, 23)], rb1)
+    await_all(b1.at[pl.ds(1, 31)], rb1)
     totals = [jnp.sum(b1[8 * s : 8 * s + 8], axis=0) for s in range(3)]
     stats = decode(totals, float(2 * LCW * TILES * 8))
-    frames = []
-    for s in (2, 1, 0):
-        block = normalize(
-            projected[16 * (2 - s) : 16 * (2 - s) + 16], stats[s][0], stats[s][1], gain[...], shift[...]
-        )
-        frames += [block[0:8], block[8:16]]
-    frames[2] = jnp.where(tm == 0, frames[4], frames[2])
-    frames[3] = jnp.where(tm == 0, frames[4], frames[3])
-    frames[0] = jnp.where(tm == 1, frames[2], frames[0])
-    frames[1] = jnp.where(tm == 1, frames[2], frames[1])
-    seqs = [jnp.concatenate(frames[a : a + 4], axis=0).astype(BF) for a in range(3)]
-
-    taps = [
-        [
-            dot(seqs[0], hw[3 * b + d]) + dot(seqs[1], hw[9 + 3 * b + d]) + dot(seqs[2], hw[18 + 3 * b + d])
-            for d in range(3)
+
+    def block(s):
+        at = 16 * (2 - s)
+        return normalize(projected[at : at + 16], stats[s][0], stats[s][1], gain[...], shift[...])
+
+    now, before = block(0), block(1)
+    first = now[0:8]
+    before = [jnp.where(tm == 0, first, before[0:8]), jnp.where(tm == 0, first, before[8:16])]
+
+    def taps_of(frames):
+        seqs = [jnp.concatenate(frames[a : a + 2], axis=0).astype(BF) for a in range(3)]
+        return [
+            [
+                dot(seqs[0], hw[3 * b + d])
+                + dot(seqs[1], hw[9 + 3 * b + d])
+                + dot(seqs[2], hw[18 + 3 * b + d])
+                for d in range(3)
+            ]
+            for b in range(3)
         ]
-        for b in range(3)
-    ]
+
+    def rolled(v, by):
+        return pltpu.roll(v.reshape(2, 8, 256), by % 8, 1).reshape(16, 256)
+
+    def middles(taps):
+        for r in range(3):
+            if r == 0:
+                q = [taps[1][d] + taps[2][d] for d in range(3)]
+            elif r == 1:
+                q = [taps[0][d] + taps[1][d] + taps[2][d] for d in range(3)]
+            else:
+                q = [taps[0][d] + taps[1][d] for d in range(3)]
+            right = q[1] + q[2]
+            left = q[0] + q[1]
+            whole = left + q[2]
+            for k in range(3):
+                m = masks[k]
+                yield k, r, 0, rolled(m * q[0], 1) + m * right
+                yield k, r, 1, m * whole
+                yield k, r, 2, m * left + rolled(m * q[2], -1)
+
     sums = jnp.zeros((8, 256), F32)
     squares = jnp.zeros((8, 256), F32)
-
-    def rolled(v, by):
-        return pltpu.roll(v.reshape(4, 8, 256), by % 8, 1).reshape(32, 256)
-
-    for r in range(3):
-        if r == 0:
-            q = [taps[1][d] + taps[2][d] for d in range(3)]
-        elif r == 1:
-            q = [taps[0][d] + taps[1][d] + taps[2][d] for d in range(3)]
-        else:
-            q = [taps[0][d] + taps[1][d] for d in range(3)]
-        right = q[1] + q[2]
-        left = q[0] + q[1]
-        whole = left + q[2]
-        for k in range(3):
-            m = masks[k]
-            kinds = (
-                rolled(m * q[0], 1) + m * right,
-                m * whole,
-                m * left + rolled(m * q[2], -1),
-            )
-            for p in range(3):
-                mid_ref[k * 9 + r * 3 + p] = kinds[p]
-                times = (2.0 if r == 1 else 1.0) * (2.0 if p == 1 else 1.0)
-                part = cores[k][16:32] * kinds[p][16:32]
-                square = part * kinds[p][16:32]
-                sums = sums + times * (part[0:8] + part[8:16])
-                squares = squares + times * (square[0:8] + square[8:16])
-    a2[0] = encode(jnp.sum(sums, axis=0, keepdims=True), jnp.sum(squares, axis=0, keepdims=True))
-    send_column(a2, sa2, ra2)
+    for k, r, p, value in middles(taps_of([*before, now[0:8], now[8:16]])):
+        mid_ref[k * 9 + r * 3 + p, 16:32] = value
+        times = (2.0 if r == 1 else 1.0) * (2.0 if p == 1 else 1.0)
+        part = cores[k] * value
+        square = part * value
+        sums = sums + times * (part[0:8] + part[8:16])
+        squares = squares + times * (square[0:8] + square[8:16])
+    b2[0] = encode(jnp.sum(sums, axis=0, keepdims=True), jnp.sum(squares, axis=0, keepdims=True))
+    for s, dy, dz, dx in everyone:
+        send(
+            b2.at[0], b2.at[64 * s + 8 * dy + dz * NX + dx], sb2, rb2,
+            (tile_at((y + dy) % NY, (z + dz) % NZH, (x + dx) % NX), (tm + s) % NT),
+        )
+
+    oldest = block(2)
+    oldest = [jnp.where(tm == 1, before[0], oldest[0:8]), jnp.where(tm == 1, before[0], oldest[8:16])]
+    for k, r, p, value in middles(taps_of([*oldest, *before])):
+        mid_ref[k * 9 + r * 3 + p, 0:16] = value
 
     await_all(wt.at[pl.ds(0, 3)], rw)
     for shard in ((tm + 2) % NT, (tm + 4) % NT, (tm + 6) % NT):
         send(wt.at[shard], wt.at[shard], ss, rs, sibling)
-
-    await_all(a2.at[pl.ds(1, 7)], ra2)
-    b2[0] = jnp.sum(a2[...], axis=0)
-    send_plane(b2, sb2, rb2, 2)
 
     await_all(wt.at[pl.ds(0, 4)], rs)
 
@@ -318,8 +327,8 @@
 
     lax.fori_loop(0, NT, arrange, 0)
 
-    await_all(b2.at[pl.ds(1, 15)], rb2)
-    totals = [jnp.sum(b2[8 * s : 8 * s + 8], axis=0) for s in range(2)]
+    await_all(b2.at[pl.ds(1, 127)], rb2)
+    totals = [jnp.sum(b2[64 * s : 64 * s + 64], axis=0) for s in range(2)]
     stats = decode(totals, float(2 * 16 * LCW * TILES * 8))
     params_ref[0:1] = stats[1][0]
     params_ref[1:2] = stats[1][1]
@@ -327,12 +336,11 @@
     params_ref[3:4] = stats[0][1]
     for part, sem in (
         (a1.at[pl.ds(1, 7)], sa1),
-        (b1.at[pl.ds(1, 23)], sb1),
+        (b1.at[pl.ds(1, 31)], sb1),
         (lbuf.at[pl.ds(0, 16)], sl),
         (wt.at[pl.ds(0, 3)], sw),
         (wt.at[pl.ds(0, 4)], ss),
-        (a2.at[pl.ds(1, 7)], sa2),
-        (b2.at[pl.ds(1, 15)], sb2),
+        (b2.at[pl.ds(1, 127)], sb2),
     ):
         await_all(part, sem)
 
@@ -462,11 +470,10 @@
             pltpu.VMEM((1, 128), F32),
             pltpu.VMEM((48, 16), F32),
             pltpu.VMEM((8, 1, 128), F32),
-            pltpu.VMEM((24, 1, 128), F32),
-            pltpu.VMEM((8, 1, 128), F32),
-            pltpu.VMEM((16, 1, 128), F32),
+            pltpu.VMEM((32, 1, 128), F32),
+            pltpu.VMEM((128, 1, 128), F32),
             dma((13,)),
-            *[dma] * 14,
+            *[dma] * 12,
         ],
         compiler_params=pltpu.CompilerParams(
             collective_id=0, has_side_effects=True, vmem_limit_bytes=20 * 2**20

time: 41.4 us -> 38.8 us (0.937)
  Pallas kernels: 41.3 us -> 38.6 us
    pallas_call x1, Pallas kernels: 39 us -> 36.3 us  [on_device(): pl.pallas_call(front_kernel, name='front', out_shape=(jax.ShapeDtypeStruc...]
where the time goes in v4:
time: 38.8 us; the launch traced here: 38.6 us
  Pallas kernels  38.6 us (99%)
    pallas_call x1, Pallas kernels, on_device(): pl.pallas_call(front_kernel, name='front', out_shape=(jax.ShapeDtypeStruc...  36.3 us
    pallas_call x1, Pallas kernels, on_device(): pl.pallas_call(back_kernel, name='back', out_shape=jax.ShapeDtypeStruct((...  2.32 us

profile of v4, /device:TPU:1, one launch (start us, length us, event | category | flops | bytes accessed | tf_op | source)
XLA Modules:
  0.0 38.6 jit_solution(13156924433860860107)
XLA Ops:
  0.0 36.3 %front.1 = (f32[27,32,256]{2,1,0:T(8,128)S(1)}, f32[8,256]{1,0:T(8,128)S(1)}, f32[3,16,256]{2,1,0:T(8,128)S(1)}, f32[24,8,128]{2,1,0:T(8,128)S(1)}, bf16[1152,768]{1,0:T(8,128)(2,1)S(1)}) custom-call(bf16[5,2,16]{2,1,0:T(2,128)(2,1)} %bitcast.13, bf16[16,256]{1,0:T(8,128)(2,1)} %wp_hbm.1, f32[1,256]{1,0:T(1,128)} %bitcast.14, f32[1,256]{1,0:T(1,128)} %bitcast.15, ...), custom_call_target="tpu_custom_call" | custom-call | tf_op jit(solution)/shard_map/front/pallas_call | solution.py:447
  36.3 2.3 %back.1 = bf16[2,8,40,128]{3,2,1,0:T(8,128)(2,1)} custom-call(f32[27,32,256]{2,1,0:T(8,128)S(1)} %get-tuple-element.10.mid, f32[8,256]{1,0:T(8,128)S(1)} %get-tuple-element.11.params, f32[3,16,256]{2,1,0:T(8,128)S(1)} %get-tuple-element.12.inside, f32[24,8,128]{2,1,0:T(8,128)S(1)} %get-tuple-element.13.blend, bf16[1152,768]{1,0:T(8,128)(2,1)S(1)} %get-tuple-element.14.wc), custom_call_target="tpu_custom_call" | custom-call | tf_op jit(solution)/shard_map/back/pallas_call | solution.py:491

commit v5 on v4

--- a/solution.py
+++ b/solution.py
@@ -19,29 +19,30 @@
 
 
 def exact_dot(x, ones):
-    high = x.astype(BF)
-    rest = x - high.astype(F32)
-    middle = rest.astype(BF)
-    low = (rest - middle.astype(F32)).astype(BF)
-    return dot(high, ones) + dot(middle, ones) + dot(low, ones)
+    high = x.astype(BF).astype(F32)
+    rest = x - high
+    middle = rest.astype(BF).astype(F32)
+    parts = jnp.concatenate([high, middle, rest - middle, jnp.zeros_like(x)], axis=0).astype(BF)
+    y = dot(parts, ones)
+    return y[0:8] + y[8:16] + y[16:24]
 
 
 def iota(shape, dim):
     return lax.broadcasted_iota(jnp.int32, shape, dim)
 
 
-def encode(sums, squares):
-    channel, lane = iota((256, 128), 0), iota((256, 128), 1)
-    ones = jnp.where(((channel >> 3) == (lane & 31)) & (lane < 64), 1.0, 0.0).astype(BF)
+def group_ones(shape, channel_dim):
+    channel, lane = iota(shape, channel_dim), iota(shape, 1 - channel_dim)
+    return jnp.where(((channel >> 3) == (lane & 31)) & (lane < 64), 1.0, 0.0).astype(BF)
+
+
+def encode(sums, squares, ones):
     row = iota((8, 256), 0)
-    stacked = jnp.where(row == 0, sums, jnp.where(row == 1, squares, 0.0))
-    coded = exact_dot(stacked, ones)
+    coded = exact_dot(jnp.where(row == 0, sums, jnp.where(row == 1, squares, 0.0)), ones)
     return jnp.where(iota((1, 128), 1) < 32, coded[0:1], coded[1:2])
 
 
-def decode(totals, count):
-    lane, channel = iota((128, 256), 0), iota((128, 256), 1)
-    ones = jnp.where(((channel >> 3) == (lane & 31)) & (lane < 64), 1.0, 0.0).astype(BF)
+def decode(totals, count, ones):
     row, place = iota((8, 128), 0), iota((8, 128), 1)
     stacked = jnp.zeros((8, 128), F32)
     for i, total in enumerate(totals):
@@ -50,8 +51,8 @@
     wide = exact_dot(stacked, ones)
     result = []
     for i in range(len(totals)):
-        mean = wide[2 * i : 2 * i + 1] / count
-        variance = wide[2 * i + 1 : 2 * i + 2] / count - mean * mean
+        mean = wide[2 * i : 2 * i + 1] * (1.0 / count)
+        variance = wide[2 * i + 1 : 2 * i + 2] * (1.0 / count) - mean * mean
         result.append((mean, lax.rsqrt(variance + 1e-06)))
     return result
 
@@ -96,7 +97,7 @@
     lat_hbm, wp_hbm, gain_hbm, shift_hbm, hw_hbm, fw_hbm, anchors_hbm, reach_hbm,
     gain2_hbm, shift2_hbm, bias_hbm,
     mid_ref, params_ref, inside_ref, blend_ref, wc_ref,
-    lbuf, wp, gain, shift, hw, wt, anchors, reach, gain2, shift2, bias, fl, a1, b1, b2,
+    lbuf, wp, gain, shift, hw, wt, anchors, reach, gain2, shift2, bias, fl, enc, dec, a1, b1, b2,
     local_sem, sa1, ra1, sb1, rb1, sb2, rb2, sl, rl, sw, rw, ss, rs,
 ):
     j = lax.axis_index("tile")
@@ -124,8 +125,8 @@
             )
         )
     ]
-    for load in loads:
-        load.start()
+    loads[0].start()
+    loads[1].start()
 
     column = [(tile_at((y + d) % NY, z, x), tm) for d in range(NY)]
     shifts = (0, 1, 2, -1)
@@ -157,6 +158,10 @@
     greeted += [plane_at(-1, *p) for p in plane] + column[1:] + chips + [sibling]
     for peer in greeted:
         pl.semaphore_signal(barrier, inc=1, device_id=peer, device_id_type=MESH)
+    for load in loads[2:]:
+        load.start()
+    enc[...] = group_ones((256, 128), 0)
+    dec[...] = group_ones((128, 256), 1)
 
     fl[...] = jnp.zeros_like(fl)
     loads[0].wait()
@@ -164,7 +169,7 @@
     for c in range(LCW):
         fl[pl.ds(32 + 1 + c, 2, stride=8), :] = lbuf[1 + c].astype(F32)
     own = dot(fl[32:48].astype(BF), wp[...])
-    a1[0] = encode(jnp.sum(own, axis=0, keepdims=True), jnp.sum(own * own, axis=0, keepdims=True))
+    a1[0] = encode(jnp.sum(own, axis=0, keepdims=True), jnp.sum(own * own, axis=0, keepdims=True), enc[...])
 
     pl.semaphore_wait(barrier, len(greeted))
 
@@ -217,9 +222,7 @@
     for load in loads[3:]:
         load.wait()
 
-    params_ref[4:5] = gain2[...]
-    params_ref[5:6] = shift2[...]
-    params_ref[6:7, 0:128] = bias[...]
+    params_ref[4:5, 0:128] = bias[...]
     col = 5 * j - 1 + (iota((16, 256), 0) & 7)
     local_col = iota((16, 256), 0) & 7
     masks, cores = [], []
@@ -248,7 +251,7 @@
 
     await_all(b1.at[pl.ds(1, 31)], rb1)
     totals = [jnp.sum(b1[8 * s : 8 * s + 8], axis=0) for s in range(3)]
-    stats = decode(totals, float(2 * LCW * TILES * 8))
+    stats = decode(totals, float(2 * LCW * TILES * 8), dec[...])
 
     def block(s):
         at = 16 * (2 - s)
@@ -299,7 +302,7 @@
         square = part * value
         sums = sums + times * (part[0:8] + part[8:16])
         squares = squares + times * (square[0:8] + square[8:16])
-    b2[0] = encode(jnp.sum(sums, axis=0, keepdims=True), jnp.sum(squares, axis=0, keepdims=True))
+    b2[0] = encode(jnp.sum(sums, axis=0, keepdims=True), jnp.sum(squares, axis=0, keepdims=True), enc[...])
     for s, dy, dz, dx in everyone:
         send(
             b2.at[0], b2.at[64 * s + 8 * dy + dz * NX + dx], sb2, rb2,
@@ -309,7 +312,10 @@
     oldest = block(2)
     oldest = [jnp.where(tm == 1, before[0], oldest[0:8]), jnp.where(tm == 1, before[0], oldest[8:16])]
     for k, r, p, value in middles(taps_of([*oldest, *before])):
-        mid_ref[k * 9 + r * 3 + p, 0:16] = value
+        i = k * 9 + r * 3 + p
+        start = mid_ref[i, 16:24]
+        mid_ref[i, 0:8] = jnp.where(tm == 0, start, value[0:8])
+        mid_ref[i, 8:16] = jnp.where(tm == 0, start, value[8:16])
 
     await_all(wt.at[pl.ds(0, 3)], rw)
     for shard in ((tm + 2) % NT, (tm + 4) % NT, (tm + 6) % NT):
@@ -327,13 +333,6 @@
 
     lax.fori_loop(0, NT, arrange, 0)
 
-    await_all(b2.at[pl.ds(1, 127)], rb2)
-    totals = [jnp.sum(b2[64 * s : 64 * s + 64], axis=0) for s in range(2)]
-    stats = decode(totals, float(2 * 16 * LCW * TILES * 8))
-    params_ref[0:1] = stats[1][0]
-    params_ref[1:2] = stats[1][1]
-    params_ref[2:3] = stats[0][0]
-    params_ref[3:4] = stats[0][1]
     for part, sem in (
         (a1.at[pl.ds(1, 7)], sa1),
         (b1.at[pl.ds(1, 31)], sb1),
@@ -343,24 +342,39 @@
         (b2.at[pl.ds(1, 127)], sb2),
     ):
         await_all(part, sem)
+    await_all(b2.at[pl.ds(1, 127)], rb2)
+    totals = [jnp.sum(b2[64 * s : 64 * s + 64], axis=0) for s in range(2)]
+    stats = decode(totals, float(2 * 16 * LCW * TILES * 8), dec[...])
+    for i, s in enumerate((1, 0)):
+        alpha = 0.5 * gain2[...] * stats[s][1]
+        beta = 0.5 * shift2[...] - stats[s][0] * alpha
+        if s == 0:
+            params_ref[2:3] = alpha
+            params_ref[3:4] = beta
+            alpha_before, beta_before = (
+                jnp.where(tm == 0, now_, before_) for now_, before_ in ((alpha, last[0]), (beta, last[1]))
+            )
+            params_ref[0:1] = alpha_before
+            params_ref[1:2] = beta_before
+        last = alpha, beta
 
 
 def back_kernel(
     mid, params, inside, blend, wc, out_ref, xs, prod, rows
 ):
-    tm = lax.axis_index("tm")
-    gain, shift, bias = params[4:5], params[5:6], params[6:7, 0:128]
-    for k in range(3):
-        keep = inside[k]
-        for r in range(3):
-            for p in range(3):
+    bias = params[4:5, 0:128]
+    for r in range(3):
+        for p in range(3):
+            for k in range(3):
                 values = mid[k * 9 + r * 3 + p]
-                before = normalize(values[0:16], params[0:1], params[1:2], gain, shift)
-                now = normalize(values[16:32], params[2:3], params[3:4], gain, shift)
-                now = keep * now
-                before = keep * before
-                first = jnp.concatenate([now[0:8], now[0:8]], axis=0)
-                before = jnp.where(tm == 0, first, before)
+                keep = inside[k]
+
+                def activate(v, row):
+                    half = v * params[row : row + 1] + params[row + 1 : row + 2]
+                    return keep * (half + half * jnp.tanh(half))
+
+                before = activate(values[0:16], 0)
+                now = activate(values[16:32], 2)
                 at = (r * 3 + p) * 48 + k * 16
                 xs[at : at + 16, 0:256] = before.astype(BF)
                 xs[at : at + 16, 256:512] = jnp.concatenate([before[8:16], now[0:8]], axis=0).astype(BF)
@@ -381,14 +395,15 @@
         ]
 
     for t in range(2):
+        across = {}
         for k in range(3):
             at = k * 16 + t * 8
-            across = {}
             for b in range(3):
                 for r in range(3):
                     (a0, a1, a3), (b0, b1, b3), (c0, c1, c3) = products(b, r, at)
-                    ab1, bc1 = a1 + b1, b1 + c1
-                    across[b, r] = (
+                    bc1 = b1 + c1
+                    ab1 = a1 + b1
+                    across[k, b, r] = (
                         pltpu.roll(a3, 1, 0) + (b0 + c0),
                         (a0 + b0) + c1,
                         a0 + bc1,
@@ -397,9 +412,12 @@
                         a1 + (b3 + c3),
                         (a3 + b3) + pltpu.roll(c0, 7, 0),
                     )
-            for c in range(7):
+        for c in range(7):
+            columns = (3, 4) if c == 3 else (c if c < 3 else c + 1,)
+            totals = [[None] * 7 for _ in columns]
+            for k in range(3):
                 (x0, x1, x3), (y0, y1, y3), (z0, z1, z3) = [
-                    [across[b, r][c] for r in range(3)] for b in range(3)
+                    [across[k, b, r][c] for r in range(3)] for b in range(3)
                 ]
                 xy1, yz1 = x1 + y1, y1 + z1
                 down = (
@@ -413,13 +431,12 @@
                 )
                 for r in range(7):
                     value = (down[r] + bias).astype(BF).astype(F32)
-                    for column in (3, 4) if c == 3 else (c if c < 3 else c + 1,):
-                        place = pl.ds(column, 8, stride=8)
+                    for i, column in enumerate(columns):
                         piece = value * blend[3 * column + k]
-                        if k == 0:
-                            rows[r, place, :] = piece
-                        else:
-                            rows[r, place, :] += piece
+                        totals[i][r] = piece if k == 0 else totals[i][r] + piece
+            for i, column in enumerate(columns):
+                for r in range(7):
+                    rows[r, pl.ds(column, 8, stride=8), :] = totals[i][r]
         for r in range(7):
             final = rows[r, 8:48].astype(BF)
             for big_row in (3, 4) if r == 3 else (r if r < 3 else r + 1,):
@@ -469,6 +486,8 @@
             pltpu.VMEM((1, 256), F32),
             pltpu.VMEM((1, 128), F32),
             pltpu.VMEM((48, 16), F32),
+            pltpu.VMEM((256, 128), BF),
+            pltpu.VMEM((128, 256), BF),
             pltpu.VMEM((8, 1, 128), F32),
             pltpu.VMEM((32, 1, 128), F32),
             pltpu.VMEM((128, 1, 128), F32),

time: 38.8 us -> 38.5 us (level)
  no operation moved by 1% of the time
where the time goes in v5:
time: 38.5 us; the launch traced here: 38.3 us
  Pallas kernels  38.3 us (99%)
    pallas_call x1, Pallas kernels, on_device(): pl.pallas_call(front_kernel, name='front', out_shape=(jax.ShapeDtypeStruc...  36.3 us
    pallas_call x1, Pallas kernels, on_device(): pl.pallas_call(back_kernel, name='back', out_shape=jax.ShapeDtypeStruct((...  2.03 us

profile of v5, /device:TPU:1, one launch (start us, length us, event | category | flops | bytes accessed | tf_op | source)
XLA Modules:
  0.0 38.3 jit_solution(2869091274975127086)
XLA Ops:
  0.0 36.3 %front.1 = (f32[27,32,256]{2,1,0:T(8,128)S(1)}, f32[8,256]{1,0:T(8,128)S(1)}, f32[3,16,256]{2,1,0:T(8,128)S(1)}, f32[24,8,128]{2,1,0:T(8,128)S(1)}, bf16[1152,768]{1,0:T(8,128)(2,1)S(1)}) custom-call(bf16[5,2,16]{2,1,0:T(2,128)(2,1)} %bitcast.13, bf16[16,256]{1,0:T(8,128)(2,1)} %wp_hbm.1, f32[1,256]{1,0:T(1,128)} %bitcast.14, f32[1,256]{1,0:T(1,128)} %bitcast.15, ...), custom_call_target="tpu_custom_call" | custom-call | tf_op jit(solution)/shard_map/front/pallas_call | solution.py:464
  36.3 2.0 %back.1 = bf16[2,8,40,128]{3,2,1,0:T(8,128)(2,1)} custom-call(f32[27,32,256]{2,1,0:T(8,128)S(1)} %get-tuple-element.10.mid, f32[8,256]{1,0:T(8,128)S(1)} %get-tuple-element.11.params, f32[3,16,256]{2,1,0:T(8,128)S(1)} %get-tuple-element.12.inside, f32[24,8,128]{2,1,0:T(8,128)S(1)} %get-tuple-element.13.blend, bf16[1152,768]{1,0:T(8,128)(2,1)S(1)} %get-tuple-element.14.wc), custom_call_target="tpu_custom_call" | custom-call | tf_op jit(solution)/shard_map/back/pallas_call | solution.py:510

commit v6 on v5

--- a/solution.py
+++ b/solution.py
@@ -31,8 +31,8 @@
     return lax.broadcasted_iota(jnp.int32, shape, dim)
 
 
-def group_ones(shape, channel_dim):
-    channel, lane = iota(shape, channel_dim), iota(shape, 1 - channel_dim)
+def group_ones():
+    channel, lane = iota((256, 128), 0), iota((256, 128), 1)
     return jnp.where(((channel >> 3) == (lane & 31)) & (lane < 64), 1.0, 0.0).astype(BF)
 
 
@@ -42,19 +42,22 @@
     return jnp.where(iota((1, 128), 1) < 32, coded[0:1], coded[1:2])
 
 
-def decode(totals, count, ones):
-    row, place = iota((8, 128), 0), iota((8, 128), 1)
+def decode(totals, count):
+    row, lane = iota((8, 128), 0), iota((8, 128), 1)
     stacked = jnp.zeros((8, 128), F32)
     for i, total in enumerate(totals):
-        stacked = jnp.where((row == 2 * i) & (place < 32), total, stacked)
-        stacked = jnp.where((row == 2 * i + 1) & (place >= 32), total, stacked)
-    wide = exact_dot(stacked, ones)
-    result = []
-    for i in range(len(totals)):
-        mean = wide[2 * i : 2 * i + 1] * (1.0 / count)
-        variance = wide[2 * i + 1 : 2 * i + 2] * (1.0 / count) - mean * mean
-        result.append((mean, lax.rsqrt(variance + 1e-06)))
-    return result
+        stacked = jnp.where(row == i, total, stacked)
+
+    def spread(first):
+        parts = [
+            jnp.take_along_axis(stacked, first + half + (lane >> 3), axis=1, mode="promise_in_bounds")
+            for half in (0, 16)
+        ]
+        return jnp.concatenate(parts, axis=1) * (1.0 / count)
+
+    mean = spread(0)
+    scale = lax.rsqrt(spread(32) - mean * mean + 1e-06)
+    return [(mean[i : i + 1], scale[i : i + 1]) for i in range(len(totals))]
 
 
 def normalize(values, mean, scale, gain, shift):
@@ -97,7 +100,7 @@
     lat_hbm, wp_hbm, gain_hbm, shift_hbm, hw_hbm, fw_hbm, anchors_hbm, reach_hbm,
     gain2_hbm, shift2_hbm, bias_hbm,
     mid_ref, params_ref, inside_ref, blend_ref, wc_ref,
-    lbuf, wp, gain, shift, hw, wt, anchors, reach, gain2, shift2, bias, fl, enc, dec, a1, b1, b2,
+    lbuf, wp, gain, shift, hw, wt, anchors, reach, gain2, shift2, bias, fl, enc, a1, b1, b2,
     local_sem, sa1, ra1, sb1, rb1, sb2, rb2, sl, rl, sw, rw, ss, rs,
 ):
     j = lax.axis_index("tile")
@@ -151,17 +154,16 @@
     chips = [chip_at(1), chip_at(-1), chip_at(2), chip_at(-2)]
 
     barrier = pltpu.get_barrier_semaphore()
-    greeted = []
+    greeted = [column[d] for d in (4, 3, 5, 2, 6, 1, 7)]
     for s in range(3):
         greeted.append(((j + 1) % TILES, (tm - s + NT) % NT))
         greeted.append(((j + TILES - 1) % TILES, (tm - s + NT) % NT))
-    greeted += [plane_at(-1, *p) for p in plane] + column[1:] + chips + [sibling]
+    greeted += [plane_at(-1, *p) for p in plane] + chips + [sibling]
     for peer in greeted:
         pl.semaphore_signal(barrier, inc=1, device_id=peer, device_id_type=MESH)
     for load in loads[2:]:
         load.start()
-    enc[...] = group_ones((256, 128), 0)
-    dec[...] = group_ones((128, 256), 1)
+    enc[...] = group_ones()
 
     fl[...] = jnp.zeros_like(fl)
     loads[0].wait()
@@ -251,7 +253,7 @@
 
     await_all(b1.at[pl.ds(1, 31)], rb1)
     totals = [jnp.sum(b1[8 * s : 8 * s + 8], axis=0) for s in range(3)]
-    stats = decode(totals, float(2 * LCW * TILES * 8), dec[...])
+    stats = decode(totals, float(2 * LCW * TILES * 8))
 
     def block(s):
         at = 16 * (2 - s)
@@ -344,7 +346,7 @@
         await_all(part, sem)
     await_all(b2.at[pl.ds(1, 127)], rb2)
     totals = [jnp.sum(b2[64 * s : 64 * s + 64], axis=0) for s in range(2)]
-    stats = decode(totals, float(2 * 16 * LCW * TILES * 8), dec[...])
+    stats = decode(totals, float(2 * 16 * LCW * TILES * 8))
     for i, s in enumerate((1, 0)):
         alpha = 0.5 * gain2[...] * stats[s][1]
         beta = 0.5 * shift2[...] - stats[s][0] * alpha
@@ -487,7 +489,6 @@
             pltpu.VMEM((1, 128), F32),
             pltpu.VMEM((48, 16), F32),
             pltpu.VMEM((256, 128), BF),
-            pltpu.VMEM((128, 256), BF),
             pltpu.VMEM((8, 1, 128), F32),
             pltpu.VMEM((32, 1, 128), F32),
             pltpu.VMEM((128, 1, 128), F32),

time: 38.5 us -> 38.5 us (level)
  no operation moved by 1% of the time
where the time goes in v6:
time: 38.5 us; the launch traced here: 38.4 us
  Pallas kernels  38.4 us (100%)
    pallas_call x1, Pallas kernels, on_device(): pl.pallas_call(front_kernel, name='front', out_shape=(jax.ShapeDtypeStruc...  36.3 us
    pallas_call x1, Pallas kernels, on_device(): pl.pallas_call(back_kernel, name='back', out_shape=jax.ShapeDtypeStruct((...  2.03 us

profile of v6, /device:TPU:1, one launch (start us, length us, event | category | flops | bytes accessed | tf_op | source)
XLA Modules:
  0.0 38.4 jit_solution(14054138650394286902)
XLA Ops:
  0.0 36.3 %front.1 = (f32[27,32,256]{2,1,0:T(8,128)S(1)}, f32[8,256]{1,0:T(8,128)S(1)}, f32[3,16,256]{2,1,0:T(8,128)S(1)}, f32[24,8,128]{2,1,0:T(8,128)S(1)}, bf16[1152,768]{1,0:T(8,128)(2,1)S(1)}) custom-call(bf16[5,2,16]{2,1,0:T(2,128)(2,1)} %bitcast.13, bf16[16,256]{1,0:T(8,128)(2,1)} %wp_hbm.1, f32[1,256]{1,0:T(1,128)} %bitcast.14, f32[1,256]{1,0:T(1,128)} %bitcast.15, ...), custom_call_target="tpu_custom_call" | custom-call | tf_op jit(solution)/shard_map/front/pallas_call | solution.py:466
  36.3 2.0 %back.1 = bf16[2,8,40,128]{3,2,1,0:T(8,128)(2,1)} custom-call(f32[27,32,256]{2,1,0:T(8,128)S(1)} %get-tuple-element.10.mid, f32[8,256]{1,0:T(8,128)S(1)} %get-tuple-element.11.params, f32[3,16,256]{2,1,0:T(8,128)S(1)} %get-tuple-element.12.inside, f32[24,8,128]{2,1,0:T(8,128)S(1)} %get-tuple-element.13.blend, bf16[1152,768]{1,0:T(8,128)(2,1)S(1)} %get-tuple-element.14.wc), custom_call_target="tpu_custom_call" | custom-call | tf_op jit(solution)/shard_map/back/pallas_call | solution.py:511
